TPU v7x, 256 devices: a whole 4x4x8 slice. The times are simulated.
256 devices in a mesh: sub: 64 (over z, x, core), slab: 4 (over y).
Axes of the slice: x: 4, y: 4, z: 8, core: 2. Of those that a mesh axis runs over, the one named last changes fastest.
Arguments:
- residual: float32 [64, 4, 128, 1024], P('sub', 'slab'), may hold values from -6 to 6
- inverse_slab: float32 [64, 4, 1024, 1024], P('sub', 'slab'), may hold values from -1 to 2, as said below
- diagonal: float32 [64, 4, 1024], P('sub', 'slab'), may hold values from 0.2 to 0.6
- primal_index: int32 [64, 4, 32], P('sub', 'slab'), may hold values from 0 to 1023
- coarse_map: int32 [64, 32], P('sub'), may hold values from 0 to 1023
- schur_small: float32 [64, 32, 32], P('sub'), may hold values from -1 to 2, as said below
- constraint_basis: float32 [64, 4, 32, 1024], P('sub', 'slab'), may hold values from -0.75 to 0.75
- coarse_basis: float32 [64, 4, 32, 1024], P('sub', 'slab'), may hold values from -0.75 to 0.75
- coarse_inverse: float32 [1024, 1024], P(None, 'sub'), may hold values from -1 to 2, as said below
Outputs:
- preconditioned: float32 [64, 4, 128, 1024], P('sub', 'slab')
Inputs may be any that keep to these rules, and one draw needn't show every extreme that they name: `inverse_slab`: A diagonal near 0.5 with full off-diagonal entries of moderate size. `schur_small`: A diagonal near 1 with full off-diagonal entries of moderate size. `coarse_inverse`: A diagonal near 1 with full off-diagonal entries of moderate size.
All inputs are finite; a program needn't handle non-finite values.
Results may differ from a plain program's by a relative error of at most 0.0001.
Values sent between devices are 32-bit elements; how exact they have to be, the bound alone decides.
A program may use at most 64 MiB of HBM per device.

v0:
```python
import functools

import jax
import jax.numpy as jnp
from jax import lax
from jax.experimental import pallas as pl
from jax.experimental.pallas import tpu as pltpu
from jax.sharding import Mesh
from jax.sharding import PartitionSpec as P

SUB = ("z", "x", "core")
MESH = pl.DeviceIdType.MESH
F32 = jnp.float32
BF16 = jnp.bfloat16

RHS = 128
IFACE = 1024
PRIM = 32
EXTRA = 2 * PRIM
MAIN = 16
SIDE = 32
NMAIN = RHS // MAIN
NSIDE = EXTRA // SIDE
BLOCK = 40


def split(value):
    high = value.astype(BF16)
    return high, (value - high.astype(F32)).astype(BF16)


def dot(left, right):
    return jnp.dot(left, right, preferred_element_type=F32)


def dot_t(left, right):
    return lax.dot_general(left, right, (((1,), (1,)), ((), ())), preferred_element_type=F32)


def dot3(left, right):
    rows = left.shape[0]
    left_high, left_low = split(left)
    right_high, right_low = split(right)
    both = dot(jnp.concatenate([left_high, left_low], axis=0), right_high)
    return both[:rows] + both[rows:] + dot(left_high, right_low)


def column_of(row):
    eye = lax.broadcasted_iota(jnp.int32, (PRIM, PRIM), 0) == lax.broadcasted_iota(
        jnp.int32, (PRIM, PRIM), 1
    )
    return jnp.sum(jnp.where(eye, jnp.broadcast_to(row, (PRIM, PRIM)), 0.0), axis=1, keepdims=True)


def onehot_of(column, width):
    lanes = lax.broadcasted_iota(jnp.int32, (PRIM, width), 1).astype(F32)
    return jnp.where(lanes == column, 1.0, 0.0).astype(BF16)


def kernel(
    nz, nx,
    res_ref, g_ref, diag_ref, idx_ref, map_ref, schur_ref, cb_ref, cbas_ref, cinv_ref, out_ref,
    ghi, glo, vx, r1, f1, rb1, n1, x2, r2, f2, rb2, n2, w0, gs, es, ct, gp1, gp2, yp1, yk1, yp2, yk2,
    f1_s, f1_r, b1_s, b1_r, f2_s, f2_r, b2_s, b2_r,
    gx_s, gx_r, gz_s, gz_r, gc_s, gc_r, y_s, y_r,
):
    k = lax.axis_index("slab")
    z, x, core = lax.axis_index("z"), lax.axis_index("x"), lax.axis_index("core")
    slabs = 4

    barrier = pltpu.get_barrier_semaphore()
    for d in range(1, slabs):
        pl.semaphore_signal(barrier, inc=1, device_id={"slab": lax.rem(k + d, slabs)}, device_id_type=MESH)
    for d in range(1, nx):
        pl.semaphore_signal(barrier, inc=1, device_id={"x": lax.rem(x + d, nx)}, device_id_type=MESH)
    for d in range(1, nz):
        pl.semaphore_signal(barrier, inc=1, device_id={"z": lax.rem(z + d, nz)}, device_id_type=MESH)
    pl.semaphore_signal(barrier, inc=1, device_id={"core": 1 - core}, device_id_type=MESH)

    own = (core * nz + z) * nx + x

    @pl.loop(0, IFACE // 64)
    def _(i):
        rows = pl.ds(pl.multiple_of(i * 64, 64), 64)
        high, low = split(g_ref[rows, :])
        ghi[rows, :] = high
        glo[rows, :] = low

    vx[0:RHS, :] = res_ref[...]

    @pl.when(k == 0)
    def _():
        r1[...] = jnp.zeros_like(r1)

    map_row = map_ref[...]
    map_col = column_of(map_row.astype(F32))
    owner, inner = map_row >> 4, map_row & 15
    place = (((owner & 1) * nz + (owner >> 3)) * nx + ((owner >> 1) & 3)) * 16 + inner
    place_hot = onehot_of(column_of(place.astype(F32)), IFACE)
    read_hot = onehot_of(column_of(idx_ref[...].astype(F32)), IFACE)

    quarter = cinv_ref[pl.ds(pl.multiple_of(k * 256, 256), 256), :]
    turned = quarter.T
    gs[own, 0:16, :] = turned[:, 0:128]
    gs[own, 16:32, :] = turned[:, 128:256]
    lanes = lax.broadcasted_iota(jnp.int32, (PRIM, 128), 1)
    subl = lax.broadcasted_iota(jnp.int32, (PRIM, 128), 0)
    map_lane = jnp.sum(
        jnp.where(lanes - PRIM * x == subl, jnp.broadcast_to(map_col, (PRIM, 128)), 0.0), axis=0, keepdims=True
    )
    gs[own, 32:BLOCK, :] = jnp.broadcast_to(map_lane, (8, 128))

    w0[0:PRIM, :] = -dot3(schur_ref[...], cb_ref[...])
    w0[PRIM:EXTRA, :] = cbas_ref[...]
    vx[RHS : RHS + EXTRA, :] = w0[...] * diag_ref[...]

    pl.semaphore_wait(barrier, (slabs - 1) + (nx - 1) + (nz - 1) + 1)

    def remote(src, dst, send, recv, to):
        return pltpu.make_async_remote_copy(
            src_ref=src, dst_ref=dst, send_sem=send, recv_sem=recv, device_id=to, device_id_type=MESH
        )

    up = {"slab": lax.rem(k + 1, slabs)}
    down = {"slab": lax.rem(k + slabs - 1, slabs)}

    def gather_x(buf, n):
        return [
            remote(buf.at[own], buf.at[own], gx_s.at[n, d], gx_r.at[n, d], {"x": lax.rem(x + d, nx)})
            for d in range(1, nx)
        ]

    def gather_z(buf, n):
        part = pl.ds((core * nz + z) * nx, nx)
        return [
            remote(buf.at[part], buf.at[part], gz_s.at[n, d], gz_r.at[n, d], {"z": lax.rem(z + d, nz)})
            for d in range(1, nz)
        ]

    def gather_core(buf, n):
        part = pl.ds(core * nz * nx, nz * nx)
        return [remote(buf.at[part], buf.at[part], gc_s.at[n], gc_r.at[n], {"core": 1 - core})]

    def among_slabs(buf, part, n):
        return [
            remote(buf.at[part], buf.at[part], y_s.at[n, d], y_r.at[n, d], {"slab": lax.rem(k + d, slabs)})
            for d in range(1, slabs)
        ]

    def start(copies):
        for copy in copies:
            copy.start()

    def arrived(copies):
        for copy in copies:
            copy.wait_recv()

    def sent(copies):
        for copy in copies:
            copy.wait_send()

    setup_x, setup_z, setup_c = gather_x(gs, 0), gather_z(gs, 0), gather_core(gs, 0)
    one_x, one_z, one_c = gather_x(gp1, 1), gather_z(gp1, 1), gather_core(gp1, 1)
    two_x, two_z, two_c = gather_x(gp2, 2), gather_z(gp2, 2), gather_core(gp2, 2)
    ey = among_slabs(es, pl.ds(2 * k, 2), 0)
    py1 = among_slabs(yp1, pl.ds(k, 1), 1)
    ky1 = among_slabs(yk1, pl.ds(k, 1), 2)
    py2 = among_slabs(yp2, pl.ds(k, 1), 3)
    ky2 = among_slabs(yk2, pl.ds(k, 1), 4)

    def times_g(value):
        rows = value.shape[0]
        high, low = split(value)
        both = dot(jnp.concatenate([high, low], axis=0), ghi[...])
        return both[:rows] + both[rows:] + dot(high, glo[...])

    def main_chunk(i):
        return i, pl.ds(pl.multiple_of(i * MAIN, MAIN), MAIN)

    def side_chunk(i):
        return NMAIN + i, pl.ds(pl.multiple_of(RHS + i * SIDE, SIDE), SIDE)

    def f1_copy(sem, rows):
        return remote(f1.at[rows], r1.at[rows], f1_s.at[sem], f1_r.at[sem], up)

    def b1_copy(sem, rows):
        return remote(n1.at[rows], rb1.at[rows], b1_s.at[sem], b1_r.at[sem], down)

    def f2_copy(sem, rows):
        return remote(f2.at[rows], r2.at[rows], f2_s.at[sem], f2_r.at[sem], up)

    def b2_copy(sem, rows):
        return remote(n2.at[rows], rb2.at[rows], b2_s.at[sem], b2_r.at[sem], down)

    def forward_one(sem, rows):
        @pl.when(k > 0)
        def _():
            f1_copy(sem, rows).wait_recv()

        value = times_g(vx[rows, :] + r1[rows, :])
        f1[rows, :] = value

        @pl.when(k < slabs - 1)
        def _():
            f1_copy(sem, rows).start()

        @pl.when(k == slabs - 1)
        def _():
            n1[rows, :] = value
            b1_copy(sem, rows).start()

    def backward_one(sem, rows):
        @pl.when(k < slabs - 1)
        def _():
            b1_copy(sem, rows).wait_recv()
            n1[rows, :] = f1[rows, :] + times_g(rb1[rows, :])

            @pl.when(k > 0)
            def _():
                b1_copy(sem, rows).start()

    def forward_two(sem, rows):
        @pl.when(k > 0)
        def _():
            f2_copy(sem, rows).wait_recv()
            value = times_g(x2[rows, :] + r2[rows, :])
            f2[rows, :] = value

            @pl.when(k < slabs - 1)
            def _():
                f2_copy(sem, rows).start()

            @pl.when(k == slabs - 1)
            def _():
                n2[rows, :] = value
                b2_copy(sem, rows).start()

    def backward_two(sem, rows):
        @pl.when(k < slabs - 1)
        def _():
            b2_copy(sem, rows).wait_recv()
            n2[rows, :] = f2[rows, :] + times_g(rb2[rows, :])

            @pl.when(k > 0)
            def _():
                b2_copy(sem, rows).start()

    def over_main(step):
        @pl.loop(0, NMAIN)
        def _(i):
            step(*main_chunk(i))

    def over_side(step):
        @pl.loop(0, NSIDE)
        def _(i):
            step(*side_chunk(i))

    def between(sem, rows):
        backward_one(sem, rows)
        value = res_ref[rows, :] - diag_ref[...] * n1[rows, :]
        x2[rows, :] = value

        @pl.when(k == 0)
        def _():
            forward = times_g(value)
            f2[rows, :] = forward
            f2_copy(sem, rows).start()

    def setup_to_z():
        arrived(setup_x)
        start(setup_z)

    start(setup_x)

    @pl.when(k > 0)
    def _():
        setup_to_z()

    over_main(forward_one)

    @pl.when(k == 0)
    def _():
        setup_to_z()

    @pl.when(k != 2)
    def _():
        over_side(forward_one)

    over_main(between)

    @pl.when(k == 2)
    def _():
        over_side(forward_one)

    arrived(setup_z)
    start(setup_c)
    arrived(setup_c)
    for half in range(2):
        table = gs[:, 16 * half : 16 * half + 16, :].reshape(IFACE, 128)
        high, low = split(table)
        es[2 * k + half] = dot(place_hot, high) + dot(place_hot, low)
    start(ey)

    over_side(backward_one)

    def primal_of(ref):
        high, low = split(ref[...])
        return dot_t(read_hot, high) + dot_t(read_hot, low)

    primal_one = primal_of(n1)
    yp1[k] = primal_one[:, 0:RHS]
    gp1[own] = primal_one[:, 0:RHS]
    side_primal = primal_one[:, RHS : RHS + EXTRA]
    start(py1)
    start(one_x)

    arrived(ey)
    e_high, e_low = split(jnp.concatenate([es[b] for b in range(8)], axis=1))
    e_both = jnp.concatenate([e_high, e_low], axis=0)
    depth = lax.broadcasted_iota(jnp.int32, (IFACE, 256), 0).astype(F32)

    @pl.loop(0, nz * nx * 2 // 8)
    def _(g):
        first = jnp.sum(gs[pl.ds(8 * g, 4), 32, :], axis=0, keepdims=True)
        second = jnp.sum(gs[pl.ds(8 * g + 4, 4), 32, :], axis=0, keepdims=True)
        wanted = jnp.concatenate([first, second], axis=1)
        hot = jnp.where(depth == wanted, 1.0, 0.0).astype(BF16)
        both = dot(e_both, hot)
        high, low = split(both[0:PRIM] + both[PRIM:])
        columns = pl.ds(pl.multiple_of(g * 256, 256), 256)
        ct[0:PRIM, columns] = high
        ct[PRIM:EXTRA, columns] = low

    def picked_of(buf):
        high, low = split(buf[...].reshape(nz * nx * 2 * PRIM, RHS))
        both = dot(ct[...], high)
        return both[0:PRIM] + both[PRIM:] + dot(ct[0:PRIM, :], low)

    arrived(one_x)
    start(one_z)

    over_main(forward_two)

    arrived(one_z)
    start(one_c)
    arrived(one_c)
    yk1[k] = picked_of(gp1)
    start(ky1)

    over_main(backward_two)

    arrived(py1)
    arrived(ky1)
    u1 = jnp.concatenate([jnp.sum(yp1[...], axis=0), jnp.sum(yk1[...], axis=0)], axis=0)
    primal_two = primal_of(n2) - dot3(side_primal, u1)
    yp2[k] = primal_two
    gp2[own] = primal_two
    start(two_x)
    start(py2)
    arrived(two_x)
    start(two_z)
    arrived(two_z)
    start(two_c)
    arrived(two_c)
    yk2[k] = picked_of(gp2)
    start(ky2)
    arrived(py2)
    arrived(ky2)
    u2 = jnp.concatenate([jnp.sum(yp2[...], axis=0), jnp.sum(yk2[...], axis=0)], axis=0)
    weights = jnp.concatenate([u1, u1 + u2], axis=0).T
    base = jnp.concatenate([-n1[RHS : RHS + EXTRA, :], w0[...]], axis=0)
    out_ref[...] = n1[0:RHS, :] + n2[...] + dot3(weights, base)

    for copies in (setup_x, setup_z, setup_c, one_x, one_z, one_c, two_x, two_z, two_c, ey, py1, ky1, py2, ky2):
        sent(copies)

    def sent_chunk(first):
        def step(sem, rows):
            @pl.when(k < slabs - 1)
            def _():
                (f1_copy if first else f2_copy)(sem, rows).wait_send()

            @pl.when(k > 0)
            def _():
                (b1_copy if first else b2_copy)(sem, rows).wait_send()

        return step

    over_main(sent_chunk(True))
    over_side(sent_chunk(True))
    over_main(sent_chunk(False))


def on_device(nz, nx, residual, inverse_slab, diagonal, primal_index, coarse_map, schur, basis_one, basis_two, cinv):
    subs = nz * nx * 2
    dma = pltpu.SemaphoreType.DMA
    vmem = pl.BlockSpec(memory_space=pltpu.VMEM)
    wide = lambda rows, kind=F32: pltpu.VMEM((rows, IFACE), kind)
    out = pl.pallas_call(
        functools.partial(kernel, nz, nx),
        out_shape=jax.ShapeDtypeStruct((RHS, IFACE), F32),
        in_specs=[vmem] * 9,
        out_specs=vmem,
        scratch_shapes=[
            wide(IFACE, BF16), wide(IFACE, BF16),
            *[wide(RHS + EXTRA)] * 5,
            *[wide(RHS)] * 5,
            wide(EXTRA),
            pltpu.VMEM((subs, BLOCK, 128), F32),
            pltpu.VMEM((8, PRIM, 128), F32),
            pltpu.VMEM((EXTRA, subs * PRIM), BF16),
            *[pltpu.VMEM((subs, PRIM, RHS), F32)] * 2,
            *[pltpu.VMEM((4, PRIM, RHS), F32)] * 4,
            *[dma((NMAIN + NSIDE,))] * 4,
            *[dma((NMAIN,))] * 4,
            dma((3, nx)), dma((3, nx)), dma((3, nz)), dma((3, nz)), dma((3,)), dma((3,)),
            dma((5, 4)), dma((5, 4)),
        ],
        compiler_params=pltpu.CompilerParams(
            collective_id=0, has_side_effects=True, vmem_limit_bytes=56 * 2**20
        ),
    )(
        residual[0, 0], inverse_slab[0, 0], diagonal[0], primal_index[0], coarse_map, schur[0],
        basis_one[0, 0], basis_two[0, 0], cinv,
    )
    return out[None, None]


def solution(mesh):
    nz, nx = 8, 4
    torus = Mesh(mesh.devices.reshape(nz, nx, 2, mesh.shape["slab"]), (*SUB, "slab"))
    in_specs = (
        P(SUB, "slab", None, None),
        P(SUB, "slab", None, None),
        P(SUB, "slab", None),
        P(SUB, "slab", None),
        P(SUB, None),
        P(SUB, None, None),
        P(SUB, "slab", None, None),
        P(SUB, "slab", None, None),
        P(None, SUB),
    )
    return jax.shard_map(
        functools.partial(on_device, nz, nx),
        mesh=torus,
        in_specs=in_specs,
        out_specs=P(SUB, "slab", None, None),
        check_vma=False,
    )
```

profile of v0, /device:TPU:1, one launch (start us, length us, event | category | flops | bytes accessed | tf_op | source)
XLA Modules:
  0.0 122.6 jit_solution(18356929086609263767)
XLA Ops:
  0.0 1.8 %copy.10.cinv_ref = f32[1024,16]{1,0:T(8,128)} copy(f32[1024,16]{0,1:T(8,128)} %param.17) | data formatting | bytes 131072 | tf_op args[8]
  1.8 118.9 %shard_map.91 = f32[128,1024]{1,0:T(8,128)} custom-call(f32[128,1024]{1,0:T(8,128)} %bitcast.10, f32[1024,1024]{1,0:T(8,128)} %bitcast.8, f32[1,1024]{1,0:T(1,128)} %bitcast.14, s32[1,32]{1,0:T(1,128)} %bitcast.15, s32[1,32]{1,0:T(1,128)} %map_ref.1, f32[32,32]{1,0:T(8,128)} %bitcast.13, f32[32,1024]{1,0:T(8,128)} %bitcast.11, f32[32,1024]{1,0:T(8,128)} %bitcast.12, ...), custom_call_target="tpu_custom_call" | custom-call | tf_op jit(solution)/shard_map/pallas_call | solution.py:399
  120.8 1.9 %copy.12 = f32[1,1,128,1024]{3,2,1,0:T(8,128)} copy(f32[1,1,128,1024]{3,2,1,0:T(8,128)} %bitcast.9) | data formatting | bytes 1048576
where the time goes:
time: 123 us
  Pallas kernels  119 us (97%)
  local copies, waits for them, and re-layouts  3.72 us (3%)
    pallas_call x1, Pallas kernels, on_device(): pl.pallas_call(functools.partial(kernel, nz, nx), out_shape=jax.ShapeDtyp...  119 us
    unnamed x2, local copies, waits for them, and re-layouts  3.72 us

commit v1 on v0

v1 whole, which is shorter than its diff:
```python
import functools

import jax
import jax.numpy as jnp
from jax import lax
from jax.experimental import pallas as pl
from jax.experimental.pallas import tpu as pltpu
from jax.sharding import Mesh
from jax.sharding import PartitionSpec as P

SUB = ("z", "x", "core")
MESH = pl.DeviceIdType.MESH
F32 = jnp.float32
BF16 = jnp.bfloat16

RHS = 128
IFACE = 1024
PRIM = 32
EXTRA = 2 * PRIM
SLABS = 4
MAIN = 16
SIDE = 32
NMAIN = RHS // MAIN
NSIDE = EXTRA // SIDE
BLOCK = 40
PIECES = 8


def split(value):
    high = value.astype(BF16)
    return high, (value - high.astype(F32)).astype(BF16)


def dot(left, right):
    return jnp.dot(left, right, preferred_element_type=F32)


def dot_t(left, right):
    return lax.dot_general(left, right, (((1,), (1,)), ((), ())), preferred_element_type=F32)


def three(left, right, times):
    rows = left[0].shape[0]
    both = times(jnp.concatenate(left, axis=0), right[0])
    return both[:rows] + both[rows:] + times(left[0], right[1])


def dot3(left, right):
    return three(split(left), split(right), dot)


def column_of(row):
    eye = lax.broadcasted_iota(jnp.int32, (PRIM, PRIM), 0) == lax.broadcasted_iota(
        jnp.int32, (PRIM, PRIM), 1
    )
    return jnp.sum(jnp.where(eye, jnp.broadcast_to(row, (PRIM, PRIM)), 0.0), axis=1, keepdims=True)


def onehot_of(column, width):
    lanes = lax.broadcasted_iota(jnp.int32, (PRIM, width), 1).astype(F32)
    return jnp.where(lanes == column, 1.0, 0.0).astype(BF16)


def moved(tile, source, target):
    shift = 32 * (target - source) % 128
    return pltpu.roll(tile, shift, 1) if shift else tile


def groups_of(pieces):
    group = lax.broadcasted_iota(jnp.int32, (8, 128), 1) // 32
    total = jnp.zeros((8, 128), F32)
    for target, parts in enumerate(pieces):
        value = sum(moved(tile, source, target) for tile, source in parts)
        total = jnp.where(group == target, value, total)
    return total


def folded(tiles):
    return [groups_of([[(tiles[q], t)] for q in range(4)]) for t in range(4)]


def kernel(
    nz, nx,
    res_hbm, g_hbm, cb_hbm, cbas_hbm, diag_ref, idx_ref, map_ref, schur_ref, cinv_ref, out_ref,
    g, cb, ghi, glo, vx, r1, f1, rb1, n1, x2, r2, f2, rb2, n2, w0,
    ta, tu, tr, tk, td, hot, gs, ms, es, ch, cl, pf, ps, gp, ag, u1s, xys,
    in_s, f1_s, f1_r, b1_s, b1_r, f2_s, f2_r, b2_s, b2_r, t_s, t_r,
    gx_s, gx_r, gz_s, gz_r, gc_s, gc_r, y_s, y_r,
):
    k = lax.axis_index("slab")
    z, x, core = lax.axis_index("z"), lax.axis_index("x"), lax.axis_index("core")
    blocks = 2 * nx * nz

    piece = IFACE // PIECES
    loads = [
        pltpu.make_async_copy(g_hbm.at[pl.ds(i * piece, piece)], g.at[pl.ds(i * piece, piece)], in_s.at[i])
        for i in range(PIECES)
    ]
    load_res = pltpu.make_async_copy(res_hbm, vx.at[pl.ds(0, RHS)], in_s.at[PIECES])
    load_cb = pltpu.make_async_copy(cb_hbm, cb, in_s.at[PIECES + 1])
    load_cbas = pltpu.make_async_copy(cbas_hbm, w0.at[pl.ds(PRIM, PRIM)], in_s.at[PIECES + 2])
    for copy in (*loads, load_res, load_cb, load_cbas):
        copy.start()

    barrier = pltpu.get_barrier_semaphore()
    for d in range(1, nz):
        pl.semaphore_signal(barrier, inc=1, device_id={"z": lax.rem(z + d, nz)}, device_id_type=MESH)
    for d in range(1, SLABS):
        pl.semaphore_signal(barrier, inc=1, device_id={"slab": lax.rem(k + d, SLABS)}, device_id_type=MESH)
    for d in range(1, nx):
        pl.semaphore_signal(barrier, inc=1, device_id={"x": lax.rem(x + d, nx)}, device_id_type=MESH)
    pl.semaphore_signal(barrier, inc=1, device_id={"core": 1 - core}, device_id_type=MESH)

    own = (core * nx + x) * nz + z

    @pl.when(k == 0)
    def _():
        r1[...] = jnp.zeros_like(r1)
        tr[...] = jnp.zeros_like(tr)

    map_row = map_ref[...]
    map_col = column_of(map_row.astype(F32))
    owner, inner = map_row >> 4, map_row & 15
    place = (((owner & 1) * nx + ((owner >> 1) & 3)) * nz + (owner >> 3)) * 16 + inner
    hot[0:PRIM, :] = onehot_of(column_of(place.astype(F32)), IFACE)
    hot[PRIM:EXTRA, :] = onehot_of(column_of(idx_ref[...].astype(F32)), IFACE)

    quarter = pl.ds(pl.multiple_of(k * 256, 256), 256)
    gs[own, 0:16, :] = cinv_ref[:, quarter][:, 0:128]
    gs[own, 16:32, :] = cinv_ref[:, quarter][:, 128:256]
    lanes = lax.broadcasted_iota(jnp.int32, (PRIM, 128), 1)
    subl = lax.broadcasted_iota(jnp.int32, (PRIM, 128), 0)
    spread = jnp.where(lanes - 8 * lax.rem(own, 16) == subl % 8, jnp.broadcast_to(map_col, (PRIM, 128)), 0.0)
    for t in range(4):
        gs[own, 32 + t : 33 + t, :] = jnp.sum(spread[8 * t : 8 * t + 8], axis=0, keepdims=True)
    gs[own, 36:40, :] = jnp.zeros((4, 128), F32)

    load_cb.wait()
    load_cbas.wait()
    w0[0:PRIM, :] = -dot3(schur_ref[...], cb[...])
    vx[RHS : RHS + EXTRA, :] = w0[...] * diag_ref[...]

    for i in range(PIECES):
        loads[i].wait()

        @pl.loop(0, piece // 64)
        def _(j):
            rows = pl.ds(pl.multiple_of(i * piece + j * 64, 64), 64)
            high, low = split(g[rows, :])
            ghi[rows, :] = high
            glo[rows, :] = low

    load_res.wait()
    pl.semaphore_wait(barrier, (SLABS - 1) + (nx - 1) + (nz - 1) + 1)

    def remote(src, dst, send, recv, to):
        return pltpu.make_async_remote_copy(
            src_ref=src, dst_ref=dst, send_sem=send, recv_sem=recv, device_id=to, device_id_type=MESH
        )

    up = {"slab": lax.rem(k + 1, SLABS)}
    down = {"slab": lax.rem(k + SLABS - 1, SLABS)}

    def gather_z(buf, n):
        return [
            remote(buf.at[own], buf.at[own], gz_s.at[n, d], gz_r.at[n, d], {"z": lax.rem(z + d, nz)})
            for d in range(1, nz)
        ]

    def gather_x(buf, n):
        part = pl.ds((core * nx + x) * nz, nz)
        return [
            remote(buf.at[part], buf.at[part], gx_s.at[n, d], gx_r.at[n, d], {"x": lax.rem(x + d, nx)})
            for d in range(1, nx)
        ]

    def gather_core(buf, n):
        part = pl.ds(core * nx * nz, nx * nz)
        return [remote(buf.at[part], buf.at[part], gc_s.at[n], gc_r.at[n], {"core": 1 - core})]

    def to_slabs(copy_of, n):
        made = []
        for d in range(1, SLABS):
            other = lax.rem(k + d, SLABS)
            src, dst = copy_of(other)
            made.append(remote(src, dst, y_s.at[n, d], y_r.at[n, d], {"slab": other}))
        return made

    def start(copies):
        for copy in copies:
            copy.start()

    def arrived(copies):
        for copy in copies:
            copy.wait_recv()

    def sent(copies):
        for copy in copies:
            copy.wait_send()

    setup_z, setup_x, setup_c = gather_z(gs, 2), gather_x(gs, 2), gather_core(gs, 2)
    e_part = pl.ds(2 * k, 2)
    ey = to_slabs(lambda other: (es.at[e_part], es.at[e_part]), 4)
    coarse_z = [gather_z(gp.at[n], n) for n in range(2)]
    coarse_x = [gather_x(gp.at[n], n) for n in range(2)]
    coarse_c = [gather_core(gp.at[n], n) for n in range(2)]
    fold_y = [to_slabs(lambda other: (pf.at[n, other], ps.at[n, k]), 2 * n) for n in range(2)]
    back_y = [to_slabs(lambda other: (ag.at[n, k], ag.at[n, k]), 2 * n + 1) for n in range(2)]

    def times_g(value):
        return three(split(value), (ghi[...], glo[...]), dot)

    def times_g_turned(value):
        return three(split(value), (ghi[...], glo[...]), dot_t)

    def main_chunk(i):
        return i, pl.ds(pl.multiple_of(i * MAIN, MAIN), MAIN)

    def side_chunk(i):
        return NMAIN + i, pl.ds(pl.multiple_of(RHS + i * SIDE, SIDE), SIDE)

    def f1_copy(sem, rows):
        return remote(f1.at[rows], r1.at[rows], f1_s.at[sem], f1_r.at[sem], up)

    def b1_copy(sem, rows):
        return remote(n1.at[rows], rb1.at[rows], b1_s.at[sem], b1_r.at[sem], down)

    def f2_copy(sem, rows):
        return remote(f2.at[rows], r2.at[rows], f2_s.at[sem], f2_r.at[sem], up)

    def b2_copy(sem, rows):
        return remote(n2.at[rows], rb2.at[rows], b2_s.at[sem], b2_r.at[sem], down)

    def forward_one(sem, rows):
        @pl.when(k > 0)
        def _():
            f1_copy(sem, rows).wait_recv()

        value = times_g(vx[rows, :] + r1[rows, :])
        f1[rows, :] = value

        @pl.when(k < SLABS - 1)
        def _():
            f1_copy(sem, rows).start()

        @pl.when(k == SLABS - 1)
        def _():
            n1[rows, :] = value
            b1_copy(sem, rows).start()

    def backward_one(sem, rows):
        @pl.when(k < SLABS - 1)
        def _():
            b1_copy(sem, rows).wait_recv()
            n1[rows, :] = f1[rows, :] + times_g(rb1[rows, :])

            @pl.when(k > 0)
            def _():
                b1_copy(sem, rows).start()

    def between(sem, rows):
        backward_one(sem, rows)
        value = vx[rows, :] - diag_ref[...] * n1[rows, :]
        x2[rows, :] = value

        @pl.when(k == 0)
        def _():
            f2[rows, :] = times_g(value)
            f2_copy(sem, rows).start()

    def forward_two(sem, rows):
        @pl.when(k > 0)
        def _():
            f2_copy(sem, rows).wait_recv()
            value = times_g(x2[rows, :] + r2[rows, :])
            f2[rows, :] = value

            @pl.when(k < SLABS - 1)
            def _():
                f2_copy(sem, rows).start()

            @pl.when(k == SLABS - 1)
            def _():
                n2[rows, :] = value
                b2_copy(sem, rows).start()

    def backward_two(sem, rows):
        @pl.when(k < SLABS - 1)
        def _():
            b2_copy(sem, rows).wait_recv()
            n2[rows, :] = f2[rows, :] + times_g(rb2[rows, :])

            @pl.when(k > 0)
            def _():
                b2_copy(sem, rows).start()

    def over_main(step, hooks=()):
        @pl.loop(0, NMAIN)
        def _(i):
            step(*main_chunk(i))
            for act, places in hooks:
                due = functools.reduce(jnp.logical_or, [(k == slab) & (i == at) for slab, at in places.items()])
                pl.when(due)(act)

    def over_side(step):
        @pl.loop(0, NSIDE)
        def _(i):
            step(*side_chunk(i))

    def only(slabs, *acts):
        @pl.when(functools.reduce(jnp.logical_or, [k == slab for slab in slabs]))
        def _():
            for act in acts:
                act()

    side_forward = lambda: over_side(forward_one)
    side_backward = lambda: over_side(backward_one)

    turned_up = remote(tu, tr, t_s.at[0], t_r.at[0], up)
    turned_down = remote(tk, td, t_s.at[1], t_r.at[1], down)

    def adjoint_up():
        @pl.when(k > 0)
        def _():
            turned_up.wait_recv()

        value = hot[PRIM:EXTRA, :].astype(F32) + tr[...]
        ta[...] = value
        result = times_g_turned(value)

        @pl.when(k < SLABS - 1)
        def _():
            tu[...] = result
            turned_up.start()

        @pl.when(k == SLABS - 1)
        def _():
            tk[...] = result
            turned_down.start()

    def adjoint_down():
        turned_down.wait_recv()
        tk[...] = times_g_turned(ta[...] + td[...])

        @pl.when(k > 0)
        def _():
            turned_down.start()

    def setup_z_in():
        arrived(setup_z)
        start(setup_x)

    def setup_x_in():
        arrived(setup_x)
        start(setup_c)

    def setup_core_in():
        arrived(setup_c)
        for half in range(2):
            high, low = split(gs[:, 16 * half : 16 * half + 16, :].reshape(IFACE, 128))
            es[2 * k + half] = dot(hot[0:PRIM, :], high) + dot(hot[0:PRIM, :], low)
        start(ey)

    def coarse_operator():
        arrived(ey)
        for a in range(4):
            ms[a] = jnp.sum(gs[16 * a : 16 * a + 16, 32:40, :], axis=0)
        wide = jnp.concatenate([es[b] for b in range(8)], axis=1)
        both_e = jnp.concatenate(split(wide), axis=0)
        depth = lax.broadcasted_iota(jnp.int32, (IFACE, 256), 0).astype(F32)
        for half in range(2):

            @pl.loop(0, 4)
            def _(t):
                wanted = jnp.concatenate([ms[2 * half, pl.ds(t, 1), :], ms[2 * half + 1, pl.ds(t, 1), :]], axis=1)
                both = dot(both_e, jnp.where(depth == wanted, 1.0, 0.0).astype(BF16))
                high, low = split(both[0:PRIM] + both[PRIM:])
                rows = pl.ds(pl.multiple_of(t * PRIM, PRIM), PRIM)
                ch[rows, 256 * half : 256 * half + 256] = high
                cl[rows, 256 * half : 256 * half + 256] = low

    def give_primal(n, primal):
        tiles = folded([primal[8 * t : 8 * t + 8] for t in range(4)])
        for q in range(4):
            pf[n, q] = tiles[q]
        ps[n, k] = pf[n, k]
        start(fold_y[n])

    def primal_one():
        high, low = split(n1[0:RHS, :])
        reads = hot[PRIM:EXTRA, :]
        give_primal(0, dot_t(reads, high) + dot_t(reads, low))

    def solve_sum(n):
        arrived(fold_y[n])
        total = jnp.sum(ps[n], axis=0)
        gp[n, own] = total
        ag[n, k, 0:8, :] = total
        start(coarse_z[n])

    def solve_z(n):
        arrived(coarse_z[n])
        start(coarse_x[n])

    def solve_x(n):
        arrived(coarse_x[n])
        start(coarse_c[n])

    def solve_core(n):
        arrived(coarse_c[n])
        everyone = split(gp[n].reshape(blocks * 8, 128))
        product = three((ch[...], cl[...]), everyone, dot)
        ag[n, k, 8:16, :] = groups_of(
            [[(product[32 * t + 8 * target : 32 * t + 8 * target + 8], t) for t in range(4)] for target in range(4)]
        )
        start(back_y[n])

    def solved(n):
        arrived(back_y[n])
        tiles = [ag[n, q] for q in range(4)]
        return jnp.concatenate(
            [*folded([tile[0:8] for tile in tiles]), *folded([tile[8:16] for tile in tiles])], axis=0
        )

    def adjoint_products():
        turned = split(tk[...])
        xys[:, 0:RHS] = three(turned, split(x2[...]), dot_t)
        xys[:, RHS : RHS + EXTRA] = three(turned, split(vx[RHS : RHS + EXTRA, :]), dot_t)

    def solved_one():
        u1 = solved(0)
        u1s[...] = u1
        give_primal(1, xys[:, 0:RHS] - dot3(xys[:, RHS : RHS + EXTRA], u1))

    sum0, z0, x0, core0 = (functools.partial(act, 0) for act in (solve_sum, solve_z, solve_x, solve_core))
    sum1, z1, x1, core1 = (functools.partial(act, 1) for act in (solve_sum, solve_z, solve_x, solve_core))

    start(setup_z)
    only((2, 3), setup_z_in)
    over_main(forward_one, [(setup_z_in, {0: 6, 1: 2}), (setup_x_in, {2: 6, 3: 3}), (setup_core_in, {3: 5})])
    only((1,), setup_x_in)
    only((2,), setup_core_in)
    only((0, 1, 3), adjoint_up)
    only((1,), setup_core_in)
    only((0, 1), side_forward)
    only((0,), setup_x_in, setup_core_in)
    over_main(between, [(adjoint_up, {2: 5})])
    primal_one()
    only((3,), coarse_operator)
    only((2, 3), side_forward)
    only((2,), coarse_operator)
    only((3,), adjoint_products)
    over_main(
        forward_two,
        [(adjoint_down, {2: 1}), (sum0, {2: 4, 3: 0}), (adjoint_products, {2: 5}), (z0, {2: 7, 3: 3}), (x0, {3: 6})],
    )
    only((1,), sum0, adjoint_down, coarse_operator, z0, adjoint_products, x0, core0)
    only((0,), sum0, coarse_operator, z0, adjoint_down, adjoint_products, x0, core0, solved_one)
    only((3,), core0, solved_one)
    only((2,), side_backward)
    over_main(
        backward_two,
        [
            (x0, {2: 3}),
            (core0, {2: 4}),
            (solved_one, {1: 2, 2: 6}),
            (side_backward, {0: 6, 1: 3}),
            (sum1, {0: 2, 1: 4, 2: 7}),
            (z1, {0: 5, 1: 7}),
        ],
    )
    only((3,), sum1)
    only((2, 3), z1)
    u1 = u1s[...]
    weights = jnp.concatenate([u1, u1], axis=0).T
    base = jnp.concatenate([-n1[RHS : RHS + EXTRA, :], w0[...]], axis=0)
    out_ref[...] = n1[0:RHS, :] + n2[...] + dot3(weights, base)
    x1()
    core1()
    u2 = solved(1)
    weights = jnp.concatenate([u2, jnp.zeros_like(u2)], axis=0).T
    out_ref[...] += dot3(weights[:, 0:EXTRA], w0[...])

    for copies in (
        setup_z, setup_x, setup_c, ey, *coarse_z, *coarse_x, *coarse_c, *fold_y, *back_y,
    ):
        sent(copies)

    @pl.when(k < SLABS - 1)
    def _():
        turned_up.wait_send()

    @pl.when(k > 0)
    def _():
        turned_down.wait_send()

    def sent_chunk(first):
        def step(sem, rows):
            @pl.when(k < SLABS - 1)
            def _():
                (f1_copy if first else f2_copy)(sem, rows).wait_send()

            @pl.when(k > 0)
            def _():
                (b1_copy if first else b2_copy)(sem, rows).wait_send()

        return step

    over_main(sent_chunk(True))
    over_side(sent_chunk(True))
    over_main(sent_chunk(False))


def on_device(nz, nx, residual, inverse_slab, diagonal, primal_index, coarse_map, schur, basis_one, basis_two, cinv):
    blocks = nz * nx * 2
    dma = pltpu.SemaphoreType.DMA
    vmem = pl.BlockSpec(memory_space=pltpu.VMEM)
    hbm = pl.BlockSpec(memory_space=pl.ANY)
    wide = lambda rows, kind=F32: pltpu.VMEM((rows, IFACE), kind)
    out = pl.pallas_call(
        functools.partial(kernel, nz, nx),
        out_shape=jax.ShapeDtypeStruct((RHS, IFACE), F32),
        in_specs=[hbm] * 4 + [vmem] * 5,
        out_specs=vmem,
        scratch_shapes=[
            wide(IFACE), wide(PRIM), wide(IFACE, BF16), wide(IFACE, BF16),
            *[wide(RHS + EXTRA)] * 5,
            *[wide(RHS)] * 5,
            wide(EXTRA),
            *[wide(PRIM)] * 5,
            wide(EXTRA, BF16),
            pltpu.VMEM((blocks, BLOCK, 128), F32),
            pltpu.VMEM((4, 8, 128), F32),
            pltpu.VMEM((8, PRIM, 128), F32),
            *[pltpu.VMEM((128, blocks * 8), BF16)] * 2,
            *[pltpu.VMEM((2, 4, 8, 128), F32)] * 2,
            pltpu.VMEM((2, blocks, 8, 128), F32),
            pltpu.VMEM((2, 4, 16, 128), F32),
            pltpu.VMEM((EXTRA, RHS), F32),
            pltpu.VMEM((PRIM, RHS + EXTRA), F32),
            dma((PIECES + 3,)),
            *[dma((NMAIN + NSIDE,))] * 4,
            *[dma((NMAIN,))] * 4,
            dma((2,)), dma((2,)),
            dma((3, nx)), dma((3, nx)), dma((3, nz)), dma((3, nz)), dma((3,)), dma((3,)),
            dma((5, SLABS)), dma((5, SLABS)),
        ],
        compiler_params=pltpu.CompilerParams(
            collective_id=0, has_side_effects=True, vmem_limit_bytes=56 * 2**20
        ),
    )(
        residual[0, 0], inverse_slab[0, 0], basis_one[0, 0], basis_two[0, 0], diagonal[0], primal_index[0],
        coarse_map, schur[0], cinv.T,
    )
    return out[None, None]


def solution(mesh):
    nz, nx = 8, 4
    torus = Mesh(mesh.devices.reshape(nz, nx, 2, mesh.shape["slab"]), (*SUB, "slab"))
    in_specs = (
        P(SUB, "slab", None, None),
        P(SUB, "slab", None, None),
        P(SUB, "slab", None),
        P(SUB, "slab", None),
        P(SUB, None),
        P(SUB, None, None),
        P(SUB, "slab", None, None),
        P(SUB, "slab", None, None),
        P(None, SUB),
    )
    return jax.shard_map(
        functools.partial(on_device, nz, nx),
        mesh=torus,
        in_specs=in_specs,
        out_specs=P(SUB, "slab", None, None),
        check_vma=False,
    )
```

time: 123 us -> 102 us (0.83)
  Pallas kernels: 119 us -> 99.8 us
  local copies, waits for them, and re-layouts: 3.72 us -> 1.89 us
    pallas_call x1, Pallas kernels: 119 us -> 99.8 us  [on_device(): pl.pallas_call(functools.partial(kernel, nz, nx), out_shape=jax.ShapeDtyp...]
    unnamed x2 -> x1, local copies, waits for them, and re-layouts: 3.72 us -> 1.89 us
where the time goes in v1:
time: 102 us
  Pallas kernels  99.8 us (98%)
  local copies, waits for them, and re-layouts  1.89 us (2%)
    pallas_call x1, Pallas kernels, on_device(): pl.pallas_call(functools.partial(kernel, nz, nx), out_shape=jax.ShapeDtyp...  99.8 us

profile of v1, /device:TPU:1, one launch (start us, length us, event | category | flops | bytes accessed | tf_op | source)
XLA Modules:
  0.0 101.6 jit_solution(1570699702745098732)
XLA Ops:
  0.0 99.8 %shard_map.91 = f32[128,1024]{1,0:T(8,128)} custom-call(f32[128,1024]{1,0:T(8,128)} %bitcast.11, f32[1024,1024]{1,0:T(8,128)} %bitcast.9, f32[32,1024]{1,0:T(8,128)} %bitcast.12, f32[32,1024]{1,0:T(8,128)} %bitcast.13, f32[1,1024]{1,0:T(1,128)} %bitcast.16, s32[1,32]{1,0:T(1,128)} %bitcast.17, s32[1,32]{1,0:T(1,128)} %map_ref.1, f32[32,32]{1,0:T(8,128)} %bitcast.15, ...), custom_call_target="tpu_custom_call" | custom-call | tf_op jit(solution)/shard_map/pallas_call | solution.py:520
  99.8 1.9 %copy.11 = f32[1,1,128,1024]{3,2,1,0:T(8,128)} copy(f32[1,1,128,1024]{3,2,1,0:T(8,128)} %bitcast.10) | data formatting | bytes 1048576

commit v2 on v1

--- a/solution.py
+++ b/solution.py
@@ -21,6 +21,8 @@
 MAIN = 16
 SIDE = 32
 NMAIN = RHS // MAIN
+NTURN = PRIM // MAIN
+EARLY = 3
 NSIDE = EXTRA // SIDE
 BLOCK = 40
 PIECES = 8
@@ -81,11 +83,11 @@
 
 def kernel(
     nz, nx,
-    res_hbm, g_hbm, cb_hbm, cbas_hbm, diag_ref, idx_ref, map_ref, schur_ref, cinv_ref, out_ref,
-    g, cb, ghi, glo, vx, r1, f1, rb1, n1, x2, r2, f2, rb2, n2, w0,
+    res_hbm, g_hbm, cb_hbm, cbas_hbm, diag_hbm, idx_hbm, map_hbm, schur_hbm, cinv_hbm, out_ref,
+    diag_ref, idx_ref, map_ref, schur_ref, cinv_ref, g, cb, ghi, glo, vx, r1, f1, rb1, n1, x2, r2, f2, rb2, n2, w0,
     ta, tu, tr, tk, td, hot, gs, ms, es, ch, cl, pf, ps, gp, ag, u1s, xys,
     in_s, f1_s, f1_r, b1_s, b1_r, f2_s, f2_r, b2_s, b2_r, t_s, t_r,
-    gx_s, gx_r, gz_s, gz_r, gc_s, gc_r, y_s, y_r,
+    gx_s, gx_r, gz_s, gz_r, gp_s, gp_r, gc_s, gc_r, y_s, y_r,
 ):
     k = lax.axis_index("slab")
     z, x, core = lax.axis_index("z"), lax.axis_index("x"), lax.axis_index("core")
@@ -96,19 +98,29 @@
         pltpu.make_async_copy(g_hbm.at[pl.ds(i * piece, piece)], g.at[pl.ds(i * piece, piece)], in_s.at[i])
         for i in range(PIECES)
     ]
+    small = [
+        pltpu.make_async_copy(src, dst, in_s.at[PIECES + 3 + i])
+        for i, (src, dst) in enumerate(
+            [(map_hbm, map_ref), (idx_hbm, idx_ref), (cinv_hbm, cinv_ref), (diag_hbm, diag_ref), (schur_hbm, schur_ref)]
+        )
+    ]
     load_res = pltpu.make_async_copy(res_hbm, vx.at[pl.ds(0, RHS)], in_s.at[PIECES])
     load_cb = pltpu.make_async_copy(cb_hbm, cb, in_s.at[PIECES + 1])
     load_cbas = pltpu.make_async_copy(cbas_hbm, w0.at[pl.ds(PRIM, PRIM)], in_s.at[PIECES + 2])
-    for copy in (*loads, load_res, load_cb, load_cbas):
+    for copy in (*small[:3], *loads, load_res, *small[3:], load_cb, load_cbas):
         copy.start()
 
     barrier = pltpu.get_barrier_semaphore()
-    for d in range(1, nz):
-        pl.semaphore_signal(barrier, inc=1, device_id={"z": lax.rem(z + d, nz)}, device_id_type=MESH)
+    plane = [
+        {"z": lax.rem(z + dz, nz), "x": lax.rem(x + dx, nx)}
+        for dz in sorted(range(nz), key=lambda d: -min(d, nz - d))
+        for dx in sorted(range(nx), key=lambda d: -min(d, nx - d))
+        if dz or dx
+    ]
+    for other in plane:
+        pl.semaphore_signal(barrier, inc=1, device_id=other, device_id_type=MESH)
     for d in range(1, SLABS):
         pl.semaphore_signal(barrier, inc=1, device_id={"slab": lax.rem(k + d, SLABS)}, device_id_type=MESH)
-    for d in range(1, nx):
-        pl.semaphore_signal(barrier, inc=1, device_id={"x": lax.rem(x + d, nx)}, device_id_type=MESH)
     pl.semaphore_signal(barrier, inc=1, device_id={"core": 1 - core}, device_id_type=MESH)
 
     own = (core * nx + x) * nz + z
@@ -118,6 +130,8 @@
         r1[...] = jnp.zeros_like(r1)
         tr[...] = jnp.zeros_like(tr)
 
+    for copy in small[:3]:
+        copy.wait()
     map_row = map_ref[...]
     map_col = column_of(map_row.astype(F32))
     owner, inner = map_row >> 4, map_row & 15
@@ -135,10 +149,11 @@
         gs[own, 32 + t : 33 + t, :] = jnp.sum(spread[8 * t : 8 * t + 8], axis=0, keepdims=True)
     gs[own, 36:40, :] = jnp.zeros((4, 128), F32)
 
-    load_cb.wait()
-    load_cbas.wait()
-    w0[0:PRIM, :] = -dot3(schur_ref[...], cb[...])
-    vx[RHS : RHS + EXTRA, :] = w0[...] * diag_ref[...]
+    def bases():
+        for copy in (*small[3:], load_cb, load_cbas):
+            copy.wait()
+        w0[0:PRIM, :] = -dot3(schur_ref[...], cb[...])
+        vx[RHS : RHS + EXTRA, :] = w0[...] * diag_ref[...]
 
     for i in range(PIECES):
         loads[i].wait()
@@ -151,7 +166,7 @@
             glo[rows, :] = low
 
     load_res.wait()
-    pl.semaphore_wait(barrier, (SLABS - 1) + (nx - 1) + (nz - 1) + 1)
+    pl.semaphore_wait(barrier, (SLABS - 1) + len(plane) + 1)
 
     def remote(src, dst, send, recv, to):
         return pltpu.make_async_remote_copy(
@@ -161,17 +176,22 @@
     up = {"slab": lax.rem(k + 1, SLABS)}
     down = {"slab": lax.rem(k + SLABS - 1, SLABS)}
 
-    def gather_z(buf, n):
+    def gather_z(buf):
         return [
-            remote(buf.at[own], buf.at[own], gz_s.at[n, d], gz_r.at[n, d], {"z": lax.rem(z + d, nz)})
+            remote(buf.at[own], buf.at[own], gz_s.at[d], gz_r.at[d], {"z": lax.rem(z + d, nz)})
             for d in range(1, nz)
         ]
 
-    def gather_x(buf, n):
+    def gather_x(buf):
         part = pl.ds((core * nx + x) * nz, nz)
         return [
-            remote(buf.at[part], buf.at[part], gx_s.at[n, d], gx_r.at[n, d], {"x": lax.rem(x + d, nx)})
+            remote(buf.at[part], buf.at[part], gx_s.at[d], gx_r.at[d], {"x": lax.rem(x + d, nx)})
             for d in range(1, nx)
+        ]
+
+    def gather_plane(buf, n):
+        return [
+            remote(buf.at[own], buf.at[own], gp_s.at[n, d], gp_r.at[n, d], other) for d, other in enumerate(plane)
         ]
 
     def gather_core(buf, n):
@@ -198,11 +218,10 @@
         for copy in copies:
             copy.wait_send()
 
-    setup_z, setup_x, setup_c = gather_z(gs, 2), gather_x(gs, 2), gather_core(gs, 2)
+    setup_z, setup_x, setup_c = gather_z(gs), gather_x(gs), gather_core(gs, 2)
     e_part = pl.ds(2 * k, 2)
     ey = to_slabs(lambda other: (es.at[e_part], es.at[e_part]), 4)
-    coarse_z = [gather_z(gp.at[n], n) for n in range(2)]
-    coarse_x = [gather_x(gp.at[n], n) for n in range(2)]
+    coarse_p = [gather_plane(gp.at[n], n) for n in range(2)]
     coarse_c = [gather_core(gp.at[n], n) for n in range(2)]
     fold_y = [to_slabs(lambda other: (pf.at[n, other], ps.at[n, k]), 2 * n) for n in range(2)]
     back_y = [to_slabs(lambda other: (ag.at[n, k], ag.at[n, k]), 2 * n + 1) for n in range(2)]
@@ -299,8 +318,14 @@
         def _(i):
             step(*main_chunk(i))
             for act, places in hooks:
-                due = functools.reduce(jnp.logical_or, [(k == slab) & (i == at) for slab, at in places.items()])
-                pl.when(due)(act)
+                due = functools.reduce(
+                    jnp.logical_or, [(k == slab) & (i == at) for slab, spots in places.items() for at in spots]
+                )
+                done = sum(jnp.where((k == slab) & (i > at), 1, 0) for slab, spots in places.items() for at in spots)
+
+                @pl.when(due)
+                def _():
+                    act(done)
 
     def over_side(step):
         @pl.loop(0, NSIDE)
@@ -313,38 +338,63 @@
             for act in acts:
                 act()
 
-    side_forward = lambda: over_side(forward_one)
-    side_backward = lambda: over_side(backward_one)
-
-    turned_up = remote(tu, tr, t_s.at[0], t_r.at[0], up)
-    turned_down = remote(tk, td, t_s.at[1], t_r.at[1], down)
-
-    def adjoint_up():
+    def once(act, *args):
+        return lambda *_: act(*args)
+
+    def side_forward(i):
+        forward_one(*side_chunk(i))
+
+    def side_backward(i):
+        backward_one(*side_chunk(i))
+
+    def all_side_forward():
+        over_side(forward_one)
+
+    def all_side_backward():
+        over_side(backward_one)
+
+    def turned_up(i):
+        rows = pl.ds(pl.multiple_of(i * MAIN, MAIN), MAIN)
+        return remote(tu.at[rows], tr.at[rows], t_s.at[0, i], t_r.at[0, i], up)
+
+    def turned_down(i):
+        rows = pl.ds(pl.multiple_of(i * MAIN, MAIN), MAIN)
+        return remote(tk.at[rows], td.at[rows], t_s.at[1, i], t_r.at[1, i], down)
+
+    def adjoint_up(i):
+        rows = pl.ds(pl.multiple_of(i * MAIN, MAIN), MAIN)
+
         @pl.when(k > 0)
         def _():
-            turned_up.wait_recv()
-
-        value = hot[PRIM:EXTRA, :].astype(F32) + tr[...]
-        ta[...] = value
+            turned_up(i).wait_recv()
+
+        value = hot[pl.ds(pl.multiple_of(PRIM + i * MAIN, MAIN), MAIN), :].astype(F32) + tr[rows, :]
+        ta[rows, :] = value
         result = times_g_turned(value)
 
         @pl.when(k < SLABS - 1)
         def _():
-            tu[...] = result
-            turned_up.start()
+            tu[rows, :] = result
+            turned_up(i).start()
 
         @pl.when(k == SLABS - 1)
         def _():
-            tk[...] = result
-            turned_down.start()
-
-    def adjoint_down():
-        turned_down.wait_recv()
-        tk[...] = times_g_turned(ta[...] + td[...])
+            tk[rows, :] = result
+            turned_down(i).start()
+
+    def adjoint_down(i):
+        rows = pl.ds(pl.multiple_of(i * MAIN, MAIN), MAIN)
+        turned_down(i).wait_recv()
+        tk[rows, :] = times_g_turned(ta[rows, :] + td[rows, :])
 
         @pl.when(k > 0)
         def _():
-            turned_down.start()
+            turned_down(i).start()
+
+    def all_adjoint_down():
+        @pl.loop(0, NTURN)
+        def _(i):
+            adjoint_down(i)
 
     def setup_z_in():
         arrived(setup_z)
@@ -387,23 +437,18 @@
         start(fold_y[n])
 
     def primal_one():
-        high, low = split(n1[0:RHS, :])
-        reads = hot[PRIM:EXTRA, :]
-        give_primal(0, dot_t(reads, high) + dot_t(reads, low))
+        turned = split(tk[...])
+        give_primal(0, three(turned, split(vx[0:RHS, :]), dot_t))
 
     def solve_sum(n):
         arrived(fold_y[n])
         total = jnp.sum(ps[n], axis=0)
         gp[n, own] = total
         ag[n, k, 0:8, :] = total
-        start(coarse_z[n])
-
-    def solve_z(n):
-        arrived(coarse_z[n])
-        start(coarse_x[n])
-
-    def solve_x(n):
-        arrived(coarse_x[n])
+        start(coarse_p[n])
+
+    def solve_plane(n):
+        arrived(coarse_p[n])
         start(coarse_c[n])
 
     def solve_core(n):
@@ -422,7 +467,7 @@
             [*folded([tile[0:8] for tile in tiles]), *folded([tile[8:16] for tile in tiles])], axis=0
         )
 
-    def adjoint_products():
+    def primal_two():
         turned = split(tk[...])
         xys[:, 0:RHS] = three(turned, split(x2[...]), dot_t)
         xys[:, RHS : RHS + EXTRA] = three(turned, split(vx[RHS : RHS + EXTRA, :]), dot_t)
@@ -432,67 +477,98 @@
         u1s[...] = u1
         give_primal(1, xys[:, 0:RHS] - dot3(xys[:, RHS : RHS + EXTRA], u1))
 
-    sum0, z0, x0, core0 = (functools.partial(act, 0) for act in (solve_sum, solve_z, solve_x, solve_core))
-    sum1, z1, x1, core1 = (functools.partial(act, 1) for act in (solve_sum, solve_z, solve_x, solve_core))
+    def base_of_result():
+        u1 = u1s[...]
+        weights = jnp.concatenate([u1, u1], axis=0).T
+        base = jnp.concatenate([-n1[RHS : RHS + EXTRA, :], w0[...]], axis=0)
+        out_ref[...] = n1[0:RHS, :] + dot3(weights, base)
+
+    sum0, plane0, core0 = (once(act, 0) for act in (solve_sum, solve_plane, solve_core))
+    sum1, plane1, core1 = (once(act, 1) for act in (solve_sum, solve_plane, solve_core))
+    setup_z_at, setup_x_at, setup_core_at = map(once, (setup_z_in, setup_x_in, setup_core_in))
+    primal_at, solved_at = once(primal_one), once(solved_one)
+
+    def backward_early(i):
+        backward_two(*main_chunk(i))
+
+    def backward_late(sem, rows):
+        @pl.when((k != 2) | (sem >= EARLY))
+        def _():
+            backward_two(sem, rows)
 
     start(setup_z)
+    only((1, 2, 3), bases)
     only((2, 3), setup_z_in)
-    over_main(forward_one, [(setup_z_in, {0: 6, 1: 2}), (setup_x_in, {2: 6, 3: 3}), (setup_core_in, {3: 5})])
-    only((1,), setup_x_in)
-    only((2,), setup_core_in)
-    only((0, 1, 3), adjoint_up)
-    only((1,), setup_core_in)
-    only((0, 1), side_forward)
-    only((0,), setup_x_in, setup_core_in)
-    over_main(between, [(adjoint_up, {2: 5})])
-    primal_one()
-    only((3,), coarse_operator)
-    only((2, 3), side_forward)
-    only((2,), coarse_operator)
-    only((3,), adjoint_products)
+
+    @pl.loop(0, NTURN)
+    def _(i):
+        adjoint_up(i)
+
+    only((3,), setup_x_in)
+    over_main(
+        forward_one,
+        [
+            (setup_z_at, {0: [5], 1: [0]}),
+            (setup_x_at, {1: [6], 2: [3]}),
+            (setup_core_at, {2: [4], 3: [0]}),
+            (adjoint_down, {2: [5, 6]}),
+        ],
+    )
+    only((0,), bases, all_side_forward, setup_x_in, setup_core_in)
+    only((1,), setup_core_in, all_side_forward)
+    only((0, 1), coarse_operator, all_adjoint_down)
+    only((0, 3), primal_one)
+    over_main(
+        between,
+        [(primal_at, {1: [1], 2: [2]}), (side_forward, {2: [4, 6]}), (sum0, {0: [1], 1: [6]})],
+    )
+    only((2, 3), coarse_operator)
+    only((3,), all_side_forward)
+    only((2, 3), sum0)
+    only((2,), all_side_backward)
+    primal_two()
+    only((0, 3), plane0)
+    only((0, 3), core0)
     over_main(
         forward_two,
-        [(adjoint_down, {2: 1}), (sum0, {2: 4, 3: 0}), (adjoint_products, {2: 5}), (z0, {2: 7, 3: 3}), (x0, {3: 6})],
-    )
-    only((1,), sum0, adjoint_down, coarse_operator, z0, adjoint_products, x0, core0)
-    only((0,), sum0, coarse_operator, z0, adjoint_down, adjoint_products, x0, core0, solved_one)
-    only((3,), core0, solved_one)
-    only((2,), side_backward)
+        [
+            (backward_early, {2: list(range(NMAIN - EARLY, NMAIN))}),
+            (side_backward, {1: [3]}),
+            (plane0, {1: [4], 2: [1]}),
+            (core0, {1: [5], 2: [2]}),
+            (solved_at, {2: [5], 3: [2]}),
+            (sum1, {3: [4]}),
+        ],
+    )
+    only((0, 1), solved_one)
+    only((1,), lambda: side_backward(1))
+    only((0,), all_side_backward)
+    only((0, 1), sum1)
+    only((0,), base_of_result)
     over_main(
-        backward_two,
-        [
-            (x0, {2: 3}),
-            (core0, {2: 4}),
-            (solved_one, {1: 2, 2: 6}),
-            (side_backward, {0: 6, 1: 3}),
-            (sum1, {0: 2, 1: 4, 2: 7}),
-            (z1, {0: 5, 1: 7}),
-        ],
-    )
-    only((3,), sum1)
-    only((2, 3), z1)
-    u1 = u1s[...]
-    weights = jnp.concatenate([u1, u1], axis=0).T
-    base = jnp.concatenate([-n1[RHS : RHS + EXTRA, :], w0[...]], axis=0)
-    out_ref[...] = n1[0:RHS, :] + n2[...] + dot3(weights, base)
-    x1()
-    core1()
-    u2 = solved(1)
-    weights = jnp.concatenate([u2, jnp.zeros_like(u2)], axis=0).T
-    out_ref[...] += dot3(weights[:, 0:EXTRA], w0[...])
+        backward_late,
+        [(sum1, {2: [3]}), (plane1, {0: [0], 1: [2], 2: [7]}), (core1, {0: [2], 1: [4]})],
+    )
+    only((3,), plane1)
+    only((1, 2, 3), base_of_result)
+    only((2, 3), core1)
+    weights = jnp.concatenate([solved(1), jnp.zeros((EXTRA, RHS), F32)], axis=0).T
+    out_ref[...] += n2[...] + dot3(weights[:, 0:EXTRA], w0[...])
 
     for copies in (
-        setup_z, setup_x, setup_c, ey, *coarse_z, *coarse_x, *coarse_c, *fold_y, *back_y,
+        setup_z, setup_x, setup_c, ey, *coarse_p, *coarse_c, *fold_y, *back_y,
     ):
         sent(copies)
 
-    @pl.when(k < SLABS - 1)
-    def _():
-        turned_up.wait_send()
-
-    @pl.when(k > 0)
-    def _():
-        turned_down.wait_send()
+    @pl.loop(0, NTURN)
+    def _(i):
+        @pl.when(k < SLABS - 1)
+        def _():
+            turned_up(i).wait_send()
+
+        @pl.when(k > 0)
+        def _():
+            turned_down(i).wait_send()
 
     def sent_chunk(first):
         def step(sem, rows):
@@ -520,9 +596,13 @@
     out = pl.pallas_call(
         functools.partial(kernel, nz, nx),
         out_shape=jax.ShapeDtypeStruct((RHS, IFACE), F32),
-        in_specs=[hbm] * 4 + [vmem] * 5,
+        in_specs=[hbm] * 9,
         out_specs=vmem,
         scratch_shapes=[
+            wide(1),
+            *[pltpu.VMEM((1, PRIM), jnp.int32)] * 2,
+            pltpu.VMEM((PRIM, PRIM), F32),
+            wide(IFACE // blocks),
             wide(IFACE), wide(PRIM), wide(IFACE, BF16), wide(IFACE, BF16),
             *[wide(RHS + EXTRA)] * 5,
             *[wide(RHS)] * 5,
@@ -538,11 +618,11 @@
             pltpu.VMEM((2, 4, 16, 128), F32),
             pltpu.VMEM((EXTRA, RHS), F32),
             pltpu.VMEM((PRIM, RHS + EXTRA), F32),
-            dma((PIECES + 3,)),
+            dma((PIECES + 8,)),
             *[dma((NMAIN + NSIDE,))] * 4,
             *[dma((NMAIN,))] * 4,
-            dma((2,)), dma((2,)),
-            dma((3, nx)), dma((3, nx)), dma((3, nz)), dma((3, nz)), dma((3,)), dma((3,)),
+            dma((2, NTURN)), dma((2, NTURN)),
+            dma((nx,)), dma((nx,)), dma((nz,)), dma((nz,)), dma((2, nz * nx - 1)), dma((2, nz * nx - 1)), dma((3,)), dma((3,)),
             dma((5, SLABS)), dma((5, SLABS)),
         ],
         compiler_params=pltpu.CompilerParams(

time: 102 us -> 89.3 us (0.88)
  Pallas kernels: 99.8 us -> 87.3 us
    pallas_call x1, Pallas kernels: 99.8 us -> 87.3 us  [on_device(): pl.pallas_call(functools.partial(kernel, nz, nx), out_shape=jax.ShapeDtyp...]
where the time goes in v2:
time: 89.3 us; the launch traced here: 89.2 us
  Pallas kernels  87.3 us (98%)
  local copies, waits for them, and re-layouts  1.89 us (2%)
    pallas_call x1, Pallas kernels, on_device(): pl.pallas_call(functools.partial(kernel, nz, nx), out_shape=jax.ShapeDtyp...  87.3 us
    unnamed x1, local copies, waits for them, and re-layouts  1.89 us

profile of v2, /device:TPU:1, one launch (start us, length us, event | category | flops | bytes accessed | tf_op | source)
XLA Modules:
  0.0 89.2 jit_solution(17343056692219676031)
XLA Ops:
  0.0 87.3 %shard_map.91 = f32[128,1024]{1,0:T(8,128)} custom-call(f32[128,1024]{1,0:T(8,128)} %bitcast.11, f32[1024,1024]{1,0:T(8,128)} %bitcast.9, f32[32,1024]{1,0:T(8,128)} %bitcast.12, f32[32,1024]{1,0:T(8,128)} %bitcast.13, f32[1,1024]{1,0:T(1,128)} %bitcast.16, s32[1,32]{1,0:T(1,128)} %bitcast.17, s32[1,32]{1,0:T(1,128)} %map_hbm.1, f32[32,32]{1,0:T(8,128)} %bitcast.15, ...), custom_call_target="tpu_custom_call" | custom-call | tf_op jit(solution)/shard_map/pallas_call | solution.py:596
  87.3 1.9 %copy.11 = f32[1,1,128,1024]{3,2,1,0:T(8,128)} copy(f32[1,1,128,1024]{3,2,1,0:T(8,128)} %bitcast.10) | data formatting | bytes 1048576

commit v3 on v2

--- a/solution.py
+++ b/solution.py
@@ -18,6 +18,8 @@
 PRIM = 32
 EXTRA = 2 * PRIM
 SLABS = 4
+EARLY_Z = 4
+LEADER = (5, 2)
 MAIN = 16
 SIDE = 32
 NMAIN = RHS // MAIN
@@ -85,9 +87,9 @@
     nz, nx,
     res_hbm, g_hbm, cb_hbm, cbas_hbm, diag_hbm, idx_hbm, map_hbm, schur_hbm, cinv_hbm, out_ref,
     diag_ref, idx_ref, map_ref, schur_ref, cinv_ref, g, cb, ghi, glo, vx, r1, f1, rb1, n1, x2, r2, f2, rb2, n2, w0,
-    ta, tu, tr, tk, td, hot, gs, ms, es, ch, cl, pf, ps, gp, ag, u1s, xys,
+    ta, tu, tr, tk, td, hot, gs, ms, es, eh, ch, cl, pf, ps, gp, ag, u1s, xys,
     in_s, f1_s, f1_r, b1_s, b1_r, f2_s, f2_r, b2_s, b2_r, t_s, t_r,
-    gx_s, gx_r, gz_s, gz_r, gp_s, gp_r, gc_s, gc_r, y_s, y_r,
+    gx_s, gx_r, gz_s, gz_r, gp_s, gp_r, gc_s, gc_r, y_s, y_r, ready,
 ):
     k = lax.axis_index("slab")
     z, x, core = lax.axis_index("z"), lax.axis_index("x"), lax.axis_index("core")
@@ -117,11 +119,18 @@
         for dx in sorted(range(nx), key=lambda d: -min(d, nx - d))
         if dz or dx
     ]
-    for other in plane:
+    leads = (z == LEADER[0]) & (x == LEADER[1])
+
+    def greet(other):
         pl.semaphore_signal(barrier, inc=1, device_id=other, device_id_type=MESH)
+
     for d in range(1, SLABS):
-        pl.semaphore_signal(barrier, inc=1, device_id={"slab": lax.rem(k + d, SLABS)}, device_id_type=MESH)
-    pl.semaphore_signal(barrier, inc=1, device_id={"core": 1 - core}, device_id_type=MESH)
+        greet({"slab": lax.rem(k + d, SLABS)})
+    greet({"core": 1 - core})
+
+    @pl.when(jnp.logical_not(leads))
+    def _():
+        greet({"z": LEADER[0], "x": LEADER[1]})
 
     own = (core * nx + x) * nz + z
 
@@ -166,7 +175,20 @@
             glo[rows, :] = low
 
     load_res.wait()
-    pl.semaphore_wait(barrier, (SLABS - 1) + len(plane) + 1)
+    pl.semaphore_wait(barrier, jnp.where(leads, SLABS + len(plane), SLABS))
+
+    @pl.when(leads)
+    def _():
+        for other in plane:
+            pl.semaphore_signal(ready, inc=1, device_id=other, device_id_type=MESH)
+
+    def plane_ready():
+        @pl.when(jnp.logical_not(leads))
+        def _():
+            pl.semaphore_wait(ready, 1)
+
+        start(setup_z)
+
 
     def remote(src, dst, send, recv, to):
         return pltpu.make_async_remote_copy(
@@ -313,15 +335,21 @@
             def _():
                 b2_copy(sem, rows).start()
 
+    early = z < EARLY_Z
+
+    def here(who):
+        if isinstance(who, int):
+            return k == who
+        return (k == who[0]) & (early if who[1] else jnp.logical_not(early))
+
     def over_main(step, hooks=()):
         @pl.loop(0, NMAIN)
         def _(i):
             step(*main_chunk(i))
             for act, places in hooks:
-                due = functools.reduce(
-                    jnp.logical_or, [(k == slab) & (i == at) for slab, spots in places.items() for at in spots]
-                )
-                done = sum(jnp.where((k == slab) & (i > at), 1, 0) for slab, spots in places.items() for at in spots)
+                spots = [(here(who), at) for who, chunks in places.items() for at in chunks]
+                due = functools.reduce(jnp.logical_or, [mine & (i == at) for mine, at in spots])
+                done = sum(jnp.where(mine & (i > at), 1, 0) for mine, at in spots)
 
                 @pl.when(due)
                 def _():
@@ -332,8 +360,8 @@
         def _(i):
             step(*side_chunk(i))
 
-    def only(slabs, *acts):
-        @pl.when(functools.reduce(jnp.logical_or, [k == slab for slab in slabs]))
+    def only(those, *acts):
+        @pl.when(functools.reduce(jnp.logical_or, [here(who) for who in those]))
         def _():
             for act in acts:
                 act()
@@ -411,23 +439,29 @@
             es[2 * k + half] = dot(hot[0:PRIM, :], high) + dot(hot[0:PRIM, :], low)
         start(ey)
 
-    def coarse_operator():
+    def operator_base():
         arrived(ey)
         for a in range(4):
             ms[a] = jnp.sum(gs[16 * a : 16 * a + 16, 32:40, :], axis=0)
         wide = jnp.concatenate([es[b] for b in range(8)], axis=1)
-        both_e = jnp.concatenate(split(wide), axis=0)
+        eh[...] = jnp.concatenate(split(wide), axis=0)
+
+    def operator_piece(i):
+        t, half = i // 2, i % 2
         depth = lax.broadcasted_iota(jnp.int32, (IFACE, 256), 0).astype(F32)
-        for half in range(2):
-
-            @pl.loop(0, 4)
-            def _(t):
-                wanted = jnp.concatenate([ms[2 * half, pl.ds(t, 1), :], ms[2 * half + 1, pl.ds(t, 1), :]], axis=1)
-                both = dot(both_e, jnp.where(depth == wanted, 1.0, 0.0).astype(BF16))
-                high, low = split(both[0:PRIM] + both[PRIM:])
-                rows = pl.ds(pl.multiple_of(t * PRIM, PRIM), PRIM)
-                ch[rows, 256 * half : 256 * half + 256] = high
-                cl[rows, 256 * half : 256 * half + 256] = low
+        wanted = jnp.concatenate([ms[2 * half, pl.ds(t, 1), :], ms[2 * half + 1, pl.ds(t, 1), :]], axis=1)
+        both = dot(eh[...], jnp.where(depth == wanted, 1.0, 0.0).astype(BF16))
+        high, low = split(both[0:PRIM] + both[PRIM:])
+        rows, columns = pl.ds(pl.multiple_of(t * PRIM, PRIM), PRIM), pl.ds(pl.multiple_of(half * 256, 256), 256)
+        ch[rows, columns] = high
+        cl[rows, columns] = low
+
+    def coarse_operator():
+        operator_base()
+
+        @pl.loop(0, 8)
+        def _(i):
+            operator_piece(i)
 
     def give_primal(n, primal):
         tiles = folded([primal[8 * t : 8 * t + 8] for t in range(4)])
@@ -486,7 +520,13 @@
     sum0, plane0, core0 = (once(act, 0) for act in (solve_sum, solve_plane, solve_core))
     sum1, plane1, core1 = (once(act, 1) for act in (solve_sum, solve_plane, solve_core))
     setup_z_at, setup_x_at, setup_core_at = map(once, (setup_z_in, setup_x_in, setup_core_in))
-    primal_at, solved_at = once(primal_one), once(solved_one)
+    primal_at, solved_at, ready_at = once(primal_one), once(solved_one), once(plane_ready)
+
+    def side_backward_last():
+        side_backward(NSIDE - 1)
+
+    def operator_piece_late(i):
+        operator_piece(3 + i)
 
     def backward_early(i):
         backward_two(*main_chunk(i))
@@ -496,62 +536,77 @@
         def _():
             backward_two(sem, rows)
 
-    start(setup_z)
     only((1, 2, 3), bases)
-    only((2, 3), setup_z_in)
+    only(((1, 0), 2, 3), plane_ready)
+    only(((2, 0), (3, 0)), setup_z_in)
 
     @pl.loop(0, NTURN)
     def _(i):
         adjoint_up(i)
 
-    only((3,), setup_x_in)
+    only(((3, 1),), setup_z_in)
     over_main(
         forward_one,
         [
-            (setup_z_at, {0: [5], 1: [0]}),
-            (setup_x_at, {1: [6], 2: [3]}),
-            (setup_core_at, {2: [4], 3: [0]}),
+            (ready_at, {(0, 0): [1], (1, 1): [1]}),
+            (setup_z_at, {(1, 0): [4], (1, 1): [5], (2, 1): [3]}),
+            (setup_x_at, {(2, 0): [4], (3, 0): [0], (3, 1): [6]}),
+            (setup_core_at, {(2, 0): [6], (3, 0): [2], (3, 1): [7]}),
             (adjoint_down, {2: [5, 6]}),
         ],
     )
-    only((0,), bases, all_side_forward, setup_x_in, setup_core_in)
-    only((1,), setup_core_in, all_side_forward)
-    only((0, 1), coarse_operator, all_adjoint_down)
+    only(((0, 1),), plane_ready)
+    only((0,), bases, all_side_forward, setup_z_in, setup_x_in, setup_core_in)
+    only((1,), all_side_forward, setup_x_in)
+    only((0, 1), all_adjoint_down)
     only((0, 3), primal_one)
     over_main(
         between,
-        [(primal_at, {1: [1], 2: [2]}), (side_forward, {2: [4, 6]}), (sum0, {0: [1], 1: [6]})],
+        [
+            (primal_at, {1: [1], 2: [2]}),
+            (setup_x_at, {(2, 1): [1]}),
+            (setup_core_at, {1: [0], (2, 1): [3]}),
+            (once(operator_base), {1: [5]}),
+            (operator_piece, {1: [5, 6, 7]}),
+            (side_forward, {2: [4, 6]}),
+            (sum0, {0: [1], 1: [6]}),
+        ],
     )
-    only((2, 3), coarse_operator)
+    only((0,), coarse_operator)
     only((3,), all_side_forward)
-    only((2, 3), sum0)
+    only((2, 3), sum0, coarse_operator)
     only((2,), all_side_backward)
     primal_two()
-    only((0, 3), plane0)
-    only((0, 3), core0)
+    only((0, (3, 0)), plane0, core0)
     over_main(
         forward_two,
         [
             (backward_early, {2: list(range(NMAIN - EARLY, NMAIN))}),
+            (operator_piece_late, {1: list(range(5))}),
             (side_backward, {1: [3]}),
-            (plane0, {1: [4], 2: [1]}),
-            (core0, {1: [5], 2: [2]}),
-            (solved_at, {2: [5], 3: [2]}),
-            (sum1, {3: [4]}),
+            (plane0, {(1, 0): [4], (1, 1): [6], (2, 0): [1], (2, 1): [3], (3, 1): [0]}),
+            (core0, {(1, 0): [5], (1, 1): [7], (2, 0): [2], (2, 1): [4], (3, 1): [1]}),
+            (solved_at, {(2, 0): [6], (2, 1): [7], 3: [3]}),
+            (sum1, {(3, 0): [5], (3, 1): [6]}),
         ],
     )
+    only(((1, 1),), side_backward_last)
     only((0, 1), solved_one)
-    only((1,), lambda: side_backward(1))
+    only(((1, 0),), side_backward_last)
     only((0,), all_side_backward)
-    only((0, 1), sum1)
+    only((0, (1, 0)), sum1)
     only((0,), base_of_result)
     over_main(
         backward_late,
-        [(sum1, {2: [3]}), (plane1, {0: [0], 1: [2], 2: [7]}), (core1, {0: [2], 1: [4]})],
+        [
+            (sum1, {(1, 1): [0], (2, 0): [3], (2, 1): [4]}),
+            (plane1, {(0, 0): [2], (0, 1): [4], (1, 0): [5], (1, 1): [6], (2, 0): [7]}),
+            (core1, {(0, 0): [4], (0, 1): [5], (1, 0): [7]}),
+        ],
     )
-    only((3,), plane1)
+    only(((2, 1), 3), plane1)
     only((1, 2, 3), base_of_result)
-    only((2, 3), core1)
+    only(((1, 1), 2, 3), core1)
     weights = jnp.concatenate([solved(1), jnp.zeros((EXTRA, RHS), F32)], axis=0).T
     out_ref[...] += n2[...] + dot3(weights[:, 0:EXTRA], w0[...])
 
@@ -612,6 +667,7 @@
             pltpu.VMEM((blocks, BLOCK, 128), F32),
             pltpu.VMEM((4, 8, 128), F32),
             pltpu.VMEM((8, PRIM, 128), F32),
+            wide(EXTRA, BF16),
             *[pltpu.VMEM((128, blocks * 8), BF16)] * 2,
             *[pltpu.VMEM((2, 4, 8, 128), F32)] * 2,
             pltpu.VMEM((2, blocks, 8, 128), F32),
@@ -623,7 +679,7 @@
             *[dma((NMAIN,))] * 4,
             dma((2, NTURN)), dma((2, NTURN)),
             dma((nx,)), dma((nx,)), dma((nz,)), dma((nz,)), dma((2, nz * nx - 1)), dma((2, nz * nx - 1)), dma((3,)), dma((3,)),
-            dma((5, SLABS)), dma((5, SLABS)),
+            dma((5, SLABS)), dma((5, SLABS)), pltpu.SemaphoreType.REGULAR,
         ],
         compiler_params=pltpu.CompilerParams(
             collective_id=0, has_side_effects=True, vmem_limit_bytes=56 * 2**20

time: 89.3 us -> 87.5 us (0.980)
  Pallas kernels: 87.3 us -> 85.5 us
    pallas_call x1, Pallas kernels: 87.3 us -> 85.5 us  [on_device(): pl.pallas_call(functools.partial(kernel, nz, nx), out_shape=jax.ShapeDtyp...]
where the time goes in v3:
time: 87.5 us; the launch traced here: 87.4 us
  Pallas kernels  85.5 us (98%)
  local copies, waits for them, and re-layouts  1.89 us (2%)
    pallas_call x1, Pallas kernels, on_device(): pl.pallas_call(functools.partial(kernel, nz, nx), out_shape=jax.ShapeDtyp...  85.5 us
    unnamed x1, local copies, waits for them, and re-layouts  1.89 us

profile of v3, /device:TPU:1, one launch (start us, length us, event | category | flops | bytes accessed | tf_op | source)
XLA Modules:
  0.0 87.4 jit_solution(12954641285815759745)
XLA Ops:
  0.0 85.5 %shard_map.91 = f32[128,1024]{1,0:T(8,128)} custom-call(f32[128,1024]{1,0:T(8,128)} %bitcast.11, f32[1024,1024]{1,0:T(8,128)} %bitcast.9, f32[32,1024]{1,0:T(8,128)} %bitcast.12, f32[32,1024]{1,0:T(8,128)} %bitcast.13, f32[1,1024]{1,0:T(1,128)} %bitcast.16, s32[1,32]{1,0:T(1,128)} %bitcast.17, s32[1,32]{1,0:T(1,128)} %map_hbm.1, f32[32,32]{1,0:T(8,128)} %bitcast.15, ...), custom_call_target="tpu_custom_call" | custom-call | tf_op jit(solution)/shard_map/pallas_call | solution.py:651
  85.5 1.9 %copy.11 = f32[1,1,128,1024]{3,2,1,0:T(8,128)} copy(f32[1,1,128,1024]{3,2,1,0:T(8,128)} %bitcast.10) | data formatting | bytes 1048576

commit v4 on v3

--- a/solution.py
+++ b/solution.py
@@ -18,7 +18,7 @@
 PRIM = 32
 EXTRA = 2 * PRIM
 SLABS = 4
-EARLY_Z = 4
+EARLY_Z = 3
 LEADER = (5, 2)
 MAIN = 16
 SIDE = 32
@@ -85,10 +85,10 @@
 
 def kernel(
     nz, nx,
-    res_hbm, g_hbm, cb_hbm, cbas_hbm, diag_hbm, idx_hbm, map_hbm, schur_hbm, cinv_hbm, out_ref,
-    diag_ref, idx_ref, map_ref, schur_ref, cinv_ref, g, cb, ghi, glo, vx, r1, f1, rb1, n1, x2, r2, f2, rb2, n2, w0,
+    res_hbm, g_hbm, cb_hbm, cbas_hbm, diag_hbm, idx_hbm, map_hbm, schur_hbm, cinv_hbm, out_hbm,
+    out_ref, diag_ref, idx_ref, map_ref, schur_ref, cinv_ref, g, cb, ghi, glo, vx, r1, f1, rb1, n1, x2, r2, f2, rb2, n2, w0,
     ta, tu, tr, tk, td, hot, gs, ms, es, eh, ch, cl, pf, ps, gp, ag, u1s, xys,
-    in_s, f1_s, f1_r, b1_s, b1_r, f2_s, f2_r, b2_s, b2_r, t_s, t_r,
+    in_s, out_s, f1_s, f1_r, b1_s, b1_r, f2_s, f2_r, b2_s, b2_r, t_s, t_r,
     gx_s, gx_r, gz_s, gz_r, gp_s, gp_r, gc_s, gc_r, y_s, y_r, ready,
 ):
     k = lax.axis_index("slab")
@@ -419,11 +419,6 @@
         def _():
             turned_down(i).start()
 
-    def all_adjoint_down():
-        @pl.loop(0, NTURN)
-        def _(i):
-            adjoint_down(i)
-
     def setup_z_in():
         arrived(setup_z)
         start(setup_x)
@@ -558,18 +553,25 @@
     only(((0, 1),), plane_ready)
     only((0,), bases, all_side_forward, setup_z_in, setup_x_in, setup_core_in)
     only((1,), all_side_forward, setup_x_in)
-    only((0, 1), all_adjoint_down)
+    @pl.when(k < 2)
+    def _():
+        @pl.loop(0, NTURN)
+        def _(i):
+            adjoint_down(i)
+            pl.when(here((1, 0)) & (i == 0))(setup_core_in)
+
     only((0, 3), primal_one)
     over_main(
         between,
         [
             (primal_at, {1: [1], 2: [2]}),
             (setup_x_at, {(2, 1): [1]}),
-            (setup_core_at, {1: [0], (2, 1): [3]}),
+            (setup_core_at, {(1, 1): [0], (2, 1): [3]}),
             (once(operator_base), {1: [5]}),
             (operator_piece, {1: [5, 6, 7]}),
             (side_forward, {2: [4, 6]}),
             (sum0, {0: [1], 1: [6]}),
+            (plane0, {(0, 0): [6]}),
         ],
     )
     only((0,), coarse_operator)
@@ -577,17 +579,19 @@
     only((2, 3), sum0, coarse_operator)
     only((2,), all_side_backward)
     primal_two()
-    only((0, (3, 0)), plane0, core0)
+    only(((0, 1), (3, 0)), plane0)
+    only((0, (3, 0)), core0)
     over_main(
         forward_two,
         [
             (backward_early, {2: list(range(NMAIN - EARLY, NMAIN))}),
             (operator_piece_late, {1: list(range(5))}),
-            (side_backward, {1: [3]}),
-            (plane0, {(1, 0): [4], (1, 1): [6], (2, 0): [1], (2, 1): [3], (3, 1): [0]}),
-            (core0, {(1, 0): [5], (1, 1): [7], (2, 0): [2], (2, 1): [4], (3, 1): [1]}),
-            (solved_at, {(2, 0): [6], (2, 1): [7], 3: [3]}),
-            (sum1, {(3, 0): [5], (3, 1): [6]}),
+            (side_backward, {(1, 1): [3]}),
+            (plane0, {(1, 0): [3], (1, 1): [6], (2, 0): [1], (2, 1): [3], (3, 1): [0]}),
+            (core0, {(1, 0): [4], (1, 1): [7], (2, 0): [2], (2, 1): [4], (3, 1): [1]}),
+            (side_backward, {(1, 0): [5]}),
+            (solved_at, {(2, 0): [4], (2, 1): [6], (3, 0): [2], (3, 1): [3]}),
+            (sum1, {(2, 0): [7], (3, 0): [4], (3, 1): [6]}),
         ],
     )
     only(((1, 1),), side_backward_last)
@@ -599,19 +603,16 @@
     over_main(
         backward_late,
         [
-            (sum1, {(1, 1): [0], (2, 0): [3], (2, 1): [4]}),
-            (plane1, {(0, 0): [2], (0, 1): [4], (1, 0): [5], (1, 1): [6], (2, 0): [7]}),
-            (core1, {(0, 0): [4], (0, 1): [5], (1, 0): [7]}),
+            (sum1, {(1, 1): [1], (2, 1): [4]}),
+            (plane1, {(0, 0): [1], (0, 1): [4], (1, 0): [3], (2, 0): [7]}),
+            (core1, {(0, 0): [3], (0, 1): [5], (1, 0): [5]}),
         ],
     )
-    only(((2, 1), 3), plane1)
+    only(((1, 1), (2, 1), 3), plane1)
     only((1, 2, 3), base_of_result)
     only(((1, 1), 2, 3), core1)
-    weights = jnp.concatenate([solved(1), jnp.zeros((EXTRA, RHS), F32)], axis=0).T
-    out_ref[...] += n2[...] + dot3(weights[:, 0:EXTRA], w0[...])
-
     for copies in (
-        setup_z, setup_x, setup_c, ey, *coarse_p, *coarse_c, *fold_y, *back_y,
+        setup_z, setup_x, setup_c, ey, *coarse_p, *coarse_c, *fold_y, back_y[0],
     ):
         sent(copies)
 
@@ -641,19 +642,33 @@
     over_side(sent_chunk(True))
     over_main(sent_chunk(False))
 
+    out_ref[...] += n2[...]
+    weights = jnp.concatenate([solved(1), jnp.zeros((EXTRA, RHS), F32)], axis=0).T
+    factor = split(w0[...])
+    half = RHS // 2
+    stores = []
+    for part in range(2):
+        rows = pl.ds(part * half, half)
+        out_ref[rows, :] += three(split(weights[part * half : part * half + half, 0:EXTRA]), factor, dot)
+        stores.append(pltpu.make_async_copy(out_ref.at[rows], out_hbm.at[rows], out_s.at[part]))
+        stores[-1].start()
+    sent(back_y[1])
+    for store in stores:
+        store.wait()
+
 
 def on_device(nz, nx, residual, inverse_slab, diagonal, primal_index, coarse_map, schur, basis_one, basis_two, cinv):
     blocks = nz * nx * 2
     dma = pltpu.SemaphoreType.DMA
-    vmem = pl.BlockSpec(memory_space=pltpu.VMEM)
     hbm = pl.BlockSpec(memory_space=pl.ANY)
     wide = lambda rows, kind=F32: pltpu.VMEM((rows, IFACE), kind)
     out = pl.pallas_call(
         functools.partial(kernel, nz, nx),
         out_shape=jax.ShapeDtypeStruct((RHS, IFACE), F32),
         in_specs=[hbm] * 9,
-        out_specs=vmem,
+        out_specs=hbm,
         scratch_shapes=[
+            wide(RHS),
             wide(1),
             *[pltpu.VMEM((1, PRIM), jnp.int32)] * 2,
             pltpu.VMEM((PRIM, PRIM), F32),
@@ -674,7 +689,7 @@
             pltpu.VMEM((2, 4, 16, 128), F32),
             pltpu.VMEM((EXTRA, RHS), F32),
             pltpu.VMEM((PRIM, RHS + EXTRA), F32),
-            dma((PIECES + 8,)),
+            dma((PIECES + 8,)), dma((2,)),
             *[dma((NMAIN + NSIDE,))] * 4,
             *[dma((NMAIN,))] * 4,
             dma((2, NTURN)), dma((2, NTURN)),

time: 87.5 us -> 84.5 us (0.966)
  Pallas kernels: 85.5 us -> 82 us
    pallas_call x1, Pallas kernels: 85.5 us -> 82 us  [on_device(): pl.pallas_call(functools.partial(kernel, nz, nx), out_shape=jax.ShapeDtyp...]
where the time goes in v4:
time: 84.5 us; the launch traced here: 83.9 us
  Pallas kernels  82 us (97%)
  local copies, waits for them, and re-layouts  1.89 us (2%)
    pallas_call x1, Pallas kernels, on_device(): pl.pallas_call(functools.partial(kernel, nz, nx), out_shape=jax.ShapeDtyp...  82 us
    unnamed x1, local copies, waits for them, and re-layouts  1.89 us

profile of v4, /device:TPU:1, one launch (start us, length us, event | category | flops | bytes accessed | tf_op | source)
XLA Modules:
  0.0 83.9 jit_solution(17785641528131023760)
XLA Ops:
  0.0 82.0 %shard_map.91 = f32[128,1024]{1,0:T(8,128)} custom-call(f32[128,1024]{1,0:T(8,128)} %bitcast.11, f32[1024,1024]{1,0:T(8,128)} %bitcast.9, f32[32,1024]{1,0:T(8,128)} %bitcast.12, f32[32,1024]{1,0:T(8,128)} %bitcast.13, f32[1,1024]{1,0:T(1,128)} %bitcast.16, s32[1,32]{1,0:T(1,128)} %bitcast.17, s32[1,32]{1,0:T(1,128)} %map_hbm.1, f32[32,32]{1,0:T(8,128)} %bitcast.15, ...), custom_call_target="tpu_custom_call" | custom-call | tf_op jit(solution)/shard_map/pallas_call | solution.py:665
  82.0 1.9 %copy.11 = f32[1,1,128,1024]{3,2,1,0:T(8,128)} copy(f32[1,1,128,1024]{3,2,1,0:T(8,128)} %bitcast.10) | data formatting | bytes 1048576

commit v5 on v4

--- a/solution.py
+++ b/solution.py
@@ -198,55 +198,56 @@
     up = {"slab": lax.rem(k + 1, SLABS)}
     down = {"slab": lax.rem(k + SLABS - 1, SLABS)}
 
+    def together(copies, whole, send, recv):
+        return copies, remote(whole, whole, send, recv, down)
+
     def gather_z(buf):
-        return [
-            remote(buf.at[own], buf.at[own], gz_s.at[d], gz_r.at[d], {"z": lax.rem(z + d, nz)})
-            for d in range(1, nz)
+        copies = [
+            remote(buf.at[own], buf.at[own], gz_s.at[0], gz_r.at[0], {"z": lax.rem(z + d, nz)}) for d in range(1, nz)
         ]
+        return together(copies, buf.at[pl.ds(0, nz - 1)], gz_s.at[0], gz_r.at[0])
 
     def gather_x(buf):
         part = pl.ds((core * nx + x) * nz, nz)
-        return [
-            remote(buf.at[part], buf.at[part], gx_s.at[d], gx_r.at[d], {"x": lax.rem(x + d, nx)})
-            for d in range(1, nx)
+        copies = [
+            remote(buf.at[part], buf.at[part], gx_s.at[0], gx_r.at[0], {"x": lax.rem(x + d, nx)}) for d in range(1, nx)
         ]
+        return together(copies, buf.at[pl.ds(0, (nx - 1) * nz)], gx_s.at[0], gx_r.at[0])
 
     def gather_plane(buf, n):
-        return [
-            remote(buf.at[own], buf.at[own], gp_s.at[n, d], gp_r.at[n, d], other) for d, other in enumerate(plane)
-        ]
+        copies = [remote(buf.at[own], buf.at[own], gp_s.at[n], gp_r.at[n], other) for other in plane]
+        return together(copies, buf.at[pl.ds(0, len(plane))], gp_s.at[n], gp_r.at[n])
 
     def gather_core(buf, n):
         part = pl.ds(core * nx * nz, nx * nz)
-        return [remote(buf.at[part], buf.at[part], gc_s.at[n], gc_r.at[n], {"core": 1 - core})]
-
-    def to_slabs(copy_of, n):
-        made = []
+        copies = [remote(buf.at[part], buf.at[part], gc_s.at[n], gc_r.at[n], {"core": 1 - core})]
+        return together(copies, buf.at[part], gc_s.at[n], gc_r.at[n])
+
+    def to_slabs(copy_of, whole, n):
+        copies = []
         for d in range(1, SLABS):
             other = lax.rem(k + d, SLABS)
             src, dst = copy_of(other)
-            made.append(remote(src, dst, y_s.at[n, d], y_r.at[n, d], {"slab": other}))
-        return made
-
-    def start(copies):
-        for copy in copies:
+            copies.append(remote(src, dst, y_s.at[n], y_r.at[n], {"slab": other}))
+        return together(copies, whole, y_s.at[n], y_r.at[n])
+
+    def start(group):
+        for copy in group[0]:
             copy.start()
 
-    def arrived(copies):
-        for copy in copies:
-            copy.wait_recv()
-
-    def sent(copies):
-        for copy in copies:
-            copy.wait_send()
+    def arrived(group):
+        group[1].wait_recv()
+
+    def sent(group):
+        group[1].wait_send()
 
     setup_z, setup_x, setup_c = gather_z(gs), gather_x(gs), gather_core(gs, 2)
     e_part = pl.ds(2 * k, 2)
-    ey = to_slabs(lambda other: (es.at[e_part], es.at[e_part]), 4)
+    ey = to_slabs(lambda other: (es.at[e_part], es.at[e_part]), es.at[pl.ds(0, 6)], 4)
     coarse_p = [gather_plane(gp.at[n], n) for n in range(2)]
     coarse_c = [gather_core(gp.at[n], n) for n in range(2)]
-    fold_y = [to_slabs(lambda other: (pf.at[n, other], ps.at[n, k]), 2 * n) for n in range(2)]
-    back_y = [to_slabs(lambda other: (ag.at[n, k], ag.at[n, k]), 2 * n + 1) for n in range(2)]
+    fold_y = [to_slabs(lambda other: (pf.at[n, other], ps.at[n, k]), ps.at[n, pl.ds(0, 3)], 2 * n) for n in range(2)]
+    back_y = [to_slabs(lambda other: (ag.at[n, k], ag.at[n, k]), ag.at[n, pl.ds(0, 3)], 2 * n + 1) for n in range(2)]
 
     def times_g(value):
         return three(split(value), (ghi[...], glo[...]), dot)
@@ -261,16 +262,16 @@
         return NMAIN + i, pl.ds(pl.multiple_of(RHS + i * SIDE, SIDE), SIDE)
 
     def f1_copy(sem, rows):
-        return remote(f1.at[rows], r1.at[rows], f1_s.at[sem], f1_r.at[sem], up)
+        return remote(f1.at[rows], r1.at[rows], f1_s.at[0], f1_r.at[sem], up)
 
     def b1_copy(sem, rows):
-        return remote(n1.at[rows], rb1.at[rows], b1_s.at[sem], b1_r.at[sem], down)
+        return remote(n1.at[rows], rb1.at[rows], b1_s.at[0], b1_r.at[sem], down)
 
     def f2_copy(sem, rows):
-        return remote(f2.at[rows], r2.at[rows], f2_s.at[sem], f2_r.at[sem], up)
+        return remote(f2.at[rows], r2.at[rows], f2_s.at[0], f2_r.at[sem], up)
 
     def b2_copy(sem, rows):
-        return remote(n2.at[rows], rb2.at[rows], b2_s.at[sem], b2_r.at[sem], down)
+        return remote(n2.at[rows], rb2.at[rows], b2_s.at[0], b2_r.at[sem], down)
 
     def forward_one(sem, rows):
         @pl.when(k > 0)
@@ -383,11 +384,11 @@
 
     def turned_up(i):
         rows = pl.ds(pl.multiple_of(i * MAIN, MAIN), MAIN)
-        return remote(tu.at[rows], tr.at[rows], t_s.at[0, i], t_r.at[0, i], up)
+        return remote(tu.at[rows], tr.at[rows], t_s.at[0], t_r.at[0, i], up)
 
     def turned_down(i):
         rows = pl.ds(pl.multiple_of(i * MAIN, MAIN), MAIN)
-        return remote(tk.at[rows], td.at[rows], t_s.at[1, i], t_r.at[1, i], down)
+        return remote(tk.at[rows], td.at[rows], t_s.at[1], t_r.at[1, i], down)
 
     def adjoint_up(i):
         rows = pl.ds(pl.multiple_of(i * MAIN, MAIN), MAIN)
@@ -611,36 +612,20 @@
     only(((1, 1), (2, 1), 3), plane1)
     only((1, 2, 3), base_of_result)
     only(((1, 1), 2, 3), core1)
-    for copies in (
+    for group in (
         setup_z, setup_x, setup_c, ey, *coarse_p, *coarse_c, *fold_y, back_y[0],
     ):
-        sent(copies)
-
-    @pl.loop(0, NTURN)
-    def _(i):
-        @pl.when(k < SLABS - 1)
-        def _():
-            turned_up(i).wait_send()
-
-        @pl.when(k > 0)
-        def _():
-            turned_down(i).wait_send()
-
-    def sent_chunk(first):
-        def step(sem, rows):
-            @pl.when(k < SLABS - 1)
-            def _():
-                (f1_copy if first else f2_copy)(sem, rows).wait_send()
-
-            @pl.when(k > 0)
-            def _():
-                (b1_copy if first else b2_copy)(sem, rows).wait_send()
-
-        return step
-
-    over_main(sent_chunk(True))
-    over_side(sent_chunk(True))
-    over_main(sent_chunk(False))
+        sent(group)
+
+    @pl.when(k < SLABS - 1)
+    def _():
+        for src, dst, send, recv in ((tu, tr, t_s.at[0], t_r.at[0, 0]), (f1, r1, f1_s.at[0], f1_r.at[0]), (f2, r2, f2_s.at[0], f2_r.at[0])):
+            remote(src, dst, send, recv, up).wait_send()
+
+    @pl.when(k > 0)
+    def _():
+        for src, dst, send, recv in ((tk, td, t_s.at[1], t_r.at[1, 0]), (n1, rb1, b1_s.at[0], b1_r.at[0]), (n2, rb2, b2_s.at[0], b2_r.at[0])):
+            remote(src, dst, send, recv, down).wait_send()
 
     out_ref[...] += n2[...]
     weights = jnp.concatenate([solved(1), jnp.zeros((EXTRA, RHS), F32)], axis=0).T
@@ -690,11 +675,11 @@
             pltpu.VMEM((EXTRA, RHS), F32),
             pltpu.VMEM((PRIM, RHS + EXTRA), F32),
             dma((PIECES + 8,)), dma((2,)),
-            *[dma((NMAIN + NSIDE,))] * 4,
-            *[dma((NMAIN,))] * 4,
-            dma((2, NTURN)), dma((2, NTURN)),
-            dma((nx,)), dma((nx,)), dma((nz,)), dma((nz,)), dma((2, nz * nx - 1)), dma((2, nz * nx - 1)), dma((3,)), dma((3,)),
-            dma((5, SLABS)), dma((5, SLABS)), pltpu.SemaphoreType.REGULAR,
+            *[dma((1,)), dma((NMAIN + NSIDE,))] * 2,
+            *[dma((1,)), dma((NMAIN,))] * 2,
+            dma((2,)), dma((2, NTURN)),
+            *[dma((1,))] * 4, *[dma((2,))] * 2, *[dma((3,))] * 2,
+            dma((5,)), dma((5,)), pltpu.SemaphoreType.REGULAR,
         ],
         compiler_params=pltpu.CompilerParams(
             collective_id=0, has_side_effects=True, vmem_limit_bytes=56 * 2**20

time: 84.5 us -> 82.7 us (0.979)
  Pallas kernels: 82 us -> 80.2 us
    pallas_call x1, Pallas kernels: 82 us -> 80.2 us  [on_device(): pl.pallas_call(functools.partial(kernel, nz, nx), out_shape=jax.ShapeDtyp...]
where the time goes in v5:
time: 82.7 us; the launch traced here: 82.1 us
  Pallas kernels  80.2 us (97%)
  local copies, waits for them, and re-layouts  1.89 us (2%)
    pallas_call x1, Pallas kernels, on_device(): pl.pallas_call(functools.partial(kernel, nz, nx), out_shape=jax.ShapeDtyp...  80.2 us
    unnamed x1, local copies, waits for them, and re-layouts  1.89 us

profile of v5, /device:TPU:1, one launch (start us, length us, event | category | flops | bytes accessed | tf_op | source)
XLA Modules:
  0.0 82.1 jit_solution(9535600282500850040)
XLA Ops:
  0.0 80.2 %shard_map.91 = f32[128,1024]{1,0:T(8,128)} custom-call(f32[128,1024]{1,0:T(8,128)} %bitcast.11, f32[1024,1024]{1,0:T(8,128)} %bitcast.9, f32[32,1024]{1,0:T(8,128)} %bitcast.12, f32[32,1024]{1,0:T(8,128)} %bitcast.13, f32[1,1024]{1,0:T(1,128)} %bitcast.16, s32[1,32]{1,0:T(1,128)} %bitcast.17, s32[1,32]{1,0:T(1,128)} %map_hbm.1, f32[32,32]{1,0:T(8,128)} %bitcast.15, ...), custom_call_target="tpu_custom_call" | custom-call | tf_op jit(solution)/shard_map/pallas_call | solution.py:650
  80.2 1.9 %copy.11 = f32[1,1,128,1024]{3,2,1,0:T(8,128)} copy(f32[1,1,128,1024]{3,2,1,0:T(8,128)} %bitcast.10) | data formatting | bytes 1048576
